TPU v7x, 32 devices: a whole 2x2x4 slice. The times are simulated.
32 devices in a mesh: dp: 8 (over z, core), tensor: 4 (over y, x).
Axes of the slice: x: 2, y: 2, z: 4, core: 2. Of those that a mesh axis runs over, the one named last changes fastest.
Arguments:
- residual_in: bfloat16 [10240, 2048], P('dp'), may hold values from -6 to 6
- layer_inputs: bfloat16 [10240, 256], P('dp'), may hold values from -6 to 6
- group_ids: int32 [16], P('dp'), may hold values from 0 to 7
- cotangent: bfloat16 [10240, 2048], P('dp'), may hold values from -6 to 6
- input_gain: float32 [2048], replicated, may hold values from 0.25 to 1.75
- laurel_left: bfloat16 [2048, 64], replicated, may hold values from -0.125 to 0.125
- laurel_right: bfloat16 [64, 2048], replicated, may hold values from -0.75 to 0.75
- laurel_gain: float32 [2048], replicated, may hold values from 0.25 to 1.75
- query_weight: bfloat16 [2048, 2048], P(None, 'tensor'), may hold values from -0.125 to 0.125
- key_matrix: bfloat16 [2048, 512], replicated, may hold values from -0.125 to 0.125
- value_matrix: bfloat16 [2048, 512], replicated, may hold values from -0.125 to 0.125
- query_gain: float32 [256], replicated, may hold values from 0.25 to 1.75
- key_gain: float32 [256], replicated, may hold values from 0.25 to 1.75
- mixer_weight: bfloat16 [2048, 2048], P('tensor'), may hold values from -0.125 to 0.125
- mixer_gain: float32 [2048], replicated, may hold values from 0.25 to 1.75
- geglu_gain: float32 [2048], replicated, may hold values from 0.25 to 1.75
- gate_weight: bfloat16 [2048, 8192], P(None, 'tensor'), may hold values from -0.125 to 0.125
- up_weight: bfloat16 [2048, 8192], P(None, 'tensor'), may hold values from -0.125 to 0.125
- down_weight: bfloat16 [8192, 2048], P('tensor'), may hold values from -0.0625 to 0.0625
- output_gain: float32 [2048], replicated, may hold values from 0.25 to 1.75
- layer_gate: bfloat16 [2048, 256], replicated, may hold values from -0.125 to 0.125
- layer_project: bfloat16 [256, 2048], replicated, may hold values from -0.375 to 0.375
- layer_gain: float32 [2048], replicated, may hold values from 0.25 to 1.75
Outputs:
- output: bfloat16 [10240, 2048], P('dp')
- residual_grad: bfloat16 [10240, 2048], P('dp')
- layer_inputs_grad: bfloat16 [10240, 256], P('dp')
- input_gain_grad: float32 [2048], P('dp')
- laurel_left_grad: float32 [2048, 64], P('dp')
- laurel_right_grad: float32 [64, 2048], P(None, 'dp')
- laurel_gain_grad: float32 [2048], P('dp')
- query_weight_grad: float32 [2048, 2048], P('dp', 'tensor')
- key_weight_grad: float32 [2048, 512], P(('dp', 'tensor'))
- value_weight_grad: float32 [2048, 512], P(('dp', 'tensor'))
- query_gain_grad: float32 [256], P(('dp', 'tensor'))
- key_gain_grad: float32 [256], P(('dp', 'tensor'))
- mixer_weight_grad: float32 [2048, 2048], P('tensor', 'dp')
- mixer_gain_grad: float32 [2048], P('dp')
- geglu_gain_grad: float32 [2048], P('dp')
- gate_weight_grad: float32 [2048, 8192], P('dp', 'tensor')
- up_weight_grad: float32 [2048, 8192], P('dp', 'tensor')
- down_weight_grad: float32 [8192, 2048], P('tensor', 'dp')
- output_gain_grad: float32 [2048], P('dp')
- layer_gate_grad: float32 [2048, 256], P('dp')
- layer_project_grad: float32 [256, 2048], P(None, 'dp')
- layer_gain_grad: float32 [2048], P('dp')
Inputs may be any that keep to these rules, and one draw needn't show every extreme that they name: Continuation c follows the prompt held in dp block group_ids[c]; a prompt may have no continuation or several.
All inputs are finite; a program needn't handle non-finite values.
Results may differ from a plain program's by a relative error of at most 0.025.
Values may be sent and summed in bfloat16 or wider, within the bound.
A program may use at most 320 MiB of HBM per device.

v0:
```python
import jax
import jax.numpy as jnp
from jax import lax
from jax.sharding import PartitionSpec as P

QUERY_HEADS = 8
KEY_VALUE_HEADS = 2
P_SIZE = 1024
L = 128
CONT_DEV = 2


EPS = 1e-06
THETA = 1000000.0
INV_ROOT = 0.7071067811865476


def rms_norm(value, gain):
    return value * lax.rsqrt(jnp.mean(value * value, axis=-1, keepdims=True) + EPS) * gain


def matmul(left, right):
    return jnp.dot(left, right, preferred_element_type=jnp.float32)


def apply_rotary(values, positions):
    width = values.shape[-1]
    half = width // 2
    freqs = THETA ** (-(jnp.arange(half, dtype=jnp.float32) * 2.0 / width))
    angles = positions.astype(jnp.float32)[:, None] * freqs[None, :]
    cosine = jnp.cos(angles)[:, None, :]
    sine = jnp.sin(angles)[:, None, :]
    first = values[..., :half]
    second = values[..., half:]
    return jnp.concatenate(
        [first * cosine - second * sine, second * cosine + first * sine], axis=-1
    )


def block_positions():
    prompt_part = jnp.arange(P_SIZE, dtype=jnp.int32)
    tail_part = jnp.tile(P_SIZE + jnp.arange(L, dtype=jnp.int32), CONT_DEV)
    return jnp.concatenate([prompt_part, tail_part])


def geglu(gate, other):
    return jax.nn.gelu(gate, approximate=True) * other


def add_norm(base, branch, gain):
    return base + rms_norm(branch, gain)


def masked_scores(queries, keys, allowed):
    scale = queries.shape[-1] ** (-0.5)
    scores = jnp.einsum("qhd,kd->hqk", queries, keys, preferred_element_type=jnp.float32) * scale
    return jnp.where(allowed[None], scores, -1e30)


def attend_forward(queries, keys, values, allowed):
    scores = masked_scores(queries, keys, allowed)
    top = jnp.max(scores, axis=-1, keepdims=True)
    weights = jnp.exp(scores - top)
    totals = jnp.sum(weights, axis=-1, keepdims=True)
    probs = (weights / totals).astype(jnp.bfloat16)
    mixed = jnp.einsum("hqk,kd->qhd", probs, values, preferred_element_type=jnp.float32)
    return (mixed, top + jnp.log(totals))


def attend_backward(queries, keys, values, allowed, log_totals, grad_mixed):
    scale = queries.shape[-1] ** (-0.5)
    probs = jnp.exp(masked_scores(queries, keys, allowed) - log_totals)
    probs_low = probs.astype(jnp.bfloat16)
    grad_probs = jnp.einsum("qhd,kd->hqk", grad_mixed, values, preferred_element_type=jnp.float32)
    centre = jnp.sum(grad_probs * probs, axis=-1, keepdims=True)
    grad_scores = (probs * (grad_probs - centre)).astype(jnp.bfloat16)
    grad_queries = (
        jnp.einsum("hqk,kd->qhd", grad_scores, keys, preferred_element_type=jnp.float32) * scale
    )
    grad_keys = (
        jnp.einsum("hqk,qhd->kd", grad_scores, queries, preferred_element_type=jnp.float32) * scale
    )
    grad_values = jnp.einsum(
        "hqk,qhd->kd", probs_low, grad_mixed, preferred_element_type=jnp.float32
    )
    return (grad_queries, grad_keys, grad_values)


def on_device(
    residual_in,
    layer_inputs,
    group_ids,
    cotangent,
    input_gain,
    laurel_left,
    laurel_right,
    laurel_gain,
    query_weight,
    key_matrix,
    value_matrix,
    query_gain,
    key_gain,
    mixer_weight,
    mixer_gain,
    geglu_gain,
    gate_weight,
    up_weight,
    down_weight,
    output_gain,
    layer_gate,
    layer_project,
    layer_gain,
):
    rows = residual_in.shape[0]
    head_number = query_gain.shape[0]
    device_heads = query_weight.shape[1] // head_number
    conts = group_ids.shape[0]
    key_value_index = lax.axis_index("tensor") * device_heads // (QUERY_HEADS // KEY_VALUE_HEADS)
    positions = block_positions()
    residual = residual_in.astype(jnp.float32)
    extra = layer_inputs.astype(jnp.float32)
    normed, input_pull = jax.vjp(rms_norm, residual, input_gain)
    lowered_normed = normed.astype(jnp.bfloat16)
    laurel_inner = matmul(lowered_normed, laurel_left).astype(jnp.bfloat16)
    laurel_outer = matmul(laurel_inner, laurel_right)
    key_slice = lax.dynamic_slice_in_dim(key_matrix, key_value_index * head_number, head_number, 1)
    value_slice = lax.dynamic_slice_in_dim(
        value_matrix, key_value_index * head_number, head_number, 1
    )
    queries_raw = matmul(lowered_normed, query_weight)
    unrotated_keys = matmul(lowered_normed, key_slice)
    unrotated_values = matmul(lowered_normed, value_slice)

    def shape_heads(query_part, key_part, value_part, gain_query, gain_key):
        shaped_queries = apply_rotary(
            rms_norm(query_part.reshape(rows, device_heads, head_number), gain_query), positions
        )
        shaped_keys = apply_rotary(rms_norm(key_part, gain_key)[:, None, :], positions)[:, 0]
        shaped_values = rms_norm(value_part, 1.0)
        return (shaped_queries, shaped_keys, shaped_values)

    shaped, heads_pull = jax.vjp(
        shape_heads, queries_raw, unrotated_keys, unrotated_values, query_gain, key_gain
    )
    queries_low = shaped[0].astype(jnp.bfloat16)
    keys_low = shaped[1].astype(jnp.bfloat16)
    values_low = shaped[2].astype(jnp.bfloat16)
    prompt_keys, prompt_values = (
        lax.all_gather(keys_low[:P_SIZE], "dp", axis=0, tiled=True),
        lax.all_gather(values_low[:P_SIZE], "dp", axis=0, tiled=True),
    )
    span = prompt_keys.shape[0]
    causal_prompt = jnp.arange(P_SIZE)[:, None] >= jnp.arange(P_SIZE)[None, :]
    causal_tail = jnp.arange(L)[:, None] >= jnp.arange(L)[None, :]
    tail_allowed = jnp.concatenate([jnp.ones((L, P_SIZE), dtype=bool), causal_tail], axis=1)

    def own_prompt(whole, group):
        return lax.dynamic_slice_in_dim(whole, group * P_SIZE, P_SIZE, 0)

    own_keys = jax.vmap(own_prompt, in_axes=(None, 0))(prompt_keys, group_ids)
    own_values = jax.vmap(own_prompt, in_axes=(None, 0))(prompt_values, group_ids)
    tail_keys = jnp.concatenate(
        [own_keys, keys_low[P_SIZE:].reshape(conts, L, head_number)], axis=1
    )
    tail_values = jnp.concatenate(
        [own_values, values_low[P_SIZE:].reshape(conts, L, head_number)], axis=1
    )
    tail_queries = queries_low[P_SIZE:].reshape(conts, L, device_heads, head_number)
    prompt_mixed, prompt_lse = attend_forward(
        queries_low[:P_SIZE], keys_low[:P_SIZE], values_low[:P_SIZE], causal_prompt
    )
    tail_mixed, tail_lse = jax.vmap(attend_forward, in_axes=(0, 0, 0, None))(
        tail_queries, tail_keys, tail_values, tail_allowed
    )
    tail_mixed = tail_mixed.reshape(conts * L, device_heads, head_number)
    mixed_low = (
        jnp.concatenate([prompt_mixed, tail_mixed], axis=0)
        .reshape(rows, device_heads * head_number)
        .astype(jnp.bfloat16)
    )
    attention = lax.psum(matmul(mixed_low, mixer_weight).astype(jnp.bfloat16), "tensor").astype(
        jnp.float32
    )

    def mix_all(attended, source, normed_in, outer, gain_mixer, gain_laurel):
        return (
            rms_norm(attended, gain_mixer) + source + normed_in + rms_norm(outer, gain_laurel)
        ) * INV_ROOT

    combined, mix_pull = jax.vjp(
        mix_all, attention, residual, normed, laurel_outer, mixer_gain, laurel_gain
    )
    dense_float, pre_pull = jax.vjp(rms_norm, combined, geglu_gain)
    dense_in = dense_float.astype(jnp.bfloat16)
    gate = matmul(dense_in, gate_weight)
    upper = matmul(dense_in, up_weight)
    activation_float, geglu_pull = jax.vjp(geglu, gate, upper)
    activation = activation_float.astype(jnp.bfloat16)
    down = lax.psum(matmul(activation, down_weight).astype(jnp.bfloat16), "tensor").astype(
        jnp.float32
    )
    carried, dense_pull = jax.vjp(add_norm, combined, down, output_gain)
    carried_low = carried.astype(jnp.bfloat16)
    layer_gate_out = matmul(carried_low, layer_gate)
    layer_float, layer_pull = jax.vjp(geglu, layer_gate_out, extra)
    layer_act = layer_float.astype(jnp.bfloat16)
    layer_out = matmul(layer_act, layer_project)
    result, tail_pull = jax.vjp(add_norm, carried, layer_out, layer_gain)
    output = result.astype(jnp.bfloat16)
    grad_carried, grad_layer_out, layer_gain_grad = tail_pull(cotangent.astype(jnp.float32))
    grad_layer_low = grad_layer_out.astype(jnp.bfloat16)
    layer_project_grad = matmul(layer_act.T, grad_layer_low)
    grad_layer_act = matmul(grad_layer_low, layer_project.T)
    grad_gate_out, grad_extra = layer_pull(grad_layer_act)
    layer_inputs_grad = grad_extra.astype(jnp.bfloat16)
    grad_gate_low = grad_gate_out.astype(jnp.bfloat16)
    layer_gate_grad = matmul(carried_low.T, grad_gate_low)
    grad_carried = grad_carried + matmul(grad_gate_low, layer_gate.T)
    grad_combined, grad_down, output_gain_grad = dense_pull(grad_carried)
    grad_down_low = grad_down.astype(jnp.bfloat16)
    down_weight_grad = matmul(activation.T, grad_down_low)
    grad_activation = matmul(grad_down_low, down_weight.T)
    grad_gate, grad_upper = geglu_pull(grad_activation)
    grad_gate_low2 = grad_gate.astype(jnp.bfloat16)
    grad_upper_low = grad_upper.astype(jnp.bfloat16)
    gate_weight_grad = matmul(dense_in.T, grad_gate_low2)
    up_weight_grad = matmul(dense_in.T, grad_upper_low)
    grad_dense = lax.psum(
        (matmul(grad_gate_low2, gate_weight.T) + matmul(grad_upper_low, up_weight.T)).astype(
            jnp.bfloat16
        ),
        "tensor",
    ).astype(jnp.float32)
    grad_combined_pre, geglu_gain_grad = pre_pull(grad_dense)
    grad_combined = grad_combined + grad_combined_pre
    grad_attention, grad_source, grad_normed_mix, grad_outer, mixer_gain_grad, laurel_gain_grad = (
        mix_pull(grad_combined)
    )
    grad_attention_low = grad_attention.astype(jnp.bfloat16)
    mixer_weight_grad = matmul(mixed_low.T, grad_attention_low)
    grad_mixed = (
        matmul(grad_attention_low, mixer_weight.T)
        .astype(jnp.bfloat16)
        .reshape(rows, device_heads, head_number)
    )
    prompt_dq, prompt_dk, prompt_dv = attend_backward(
        queries_low[:P_SIZE],
        keys_low[:P_SIZE],
        values_low[:P_SIZE],
        causal_prompt,
        prompt_lse,
        grad_mixed[:P_SIZE],
    )
    tail_dq, tail_dk, tail_dv = jax.vmap(attend_backward, in_axes=(0, 0, 0, None, 0, 0))(
        tail_queries,
        tail_keys,
        tail_values,
        tail_allowed,
        tail_lse,
        grad_mixed[P_SIZE:].reshape(conts, L, device_heads, head_number),
    )
    cont_dk = tail_dk[:, :P_SIZE]
    cont_dv = tail_dv[:, :P_SIZE]
    spread_keys = jnp.zeros((span, head_number), jnp.float32)
    spread_values = jnp.zeros((span, head_number), jnp.float32)
    for index in range(conts):
        start = group_ids[index] * P_SIZE
        spread_keys = lax.dynamic_update_slice_in_dim(
            spread_keys,
            lax.dynamic_slice_in_dim(spread_keys, start, P_SIZE, 0) + cont_dk[index],
            start,
            0,
        )
        spread_values = lax.dynamic_update_slice_in_dim(
            spread_values,
            lax.dynamic_slice_in_dim(spread_values, start, P_SIZE, 0) + cont_dv[index],
            start,
            0,
        )
    owner_keys, owner_values = (
        lax.psum_scatter(
            spread_keys.astype(jnp.bfloat16), "dp", scatter_dimension=0, tiled=True
        ).astype(jnp.float32),
        lax.psum_scatter(
            spread_values.astype(jnp.bfloat16), "dp", scatter_dimension=0, tiled=True
        ).astype(jnp.float32),
    )
    grad_queries = jnp.concatenate(
        [prompt_dq, tail_dq.reshape(conts * L, device_heads, head_number)], axis=0
    )
    grad_keys = jnp.concatenate(
        [prompt_dk + owner_keys, tail_dk[:, P_SIZE:].reshape(conts * L, head_number)], axis=0
    )
    grad_values = jnp.concatenate(
        [prompt_dv + owner_values, tail_dv[:, P_SIZE:].reshape(conts * L, head_number)], axis=0
    )
    query_part, key_part, value_part, query_gain_part, key_gain_part = heads_pull(
        (grad_queries, grad_keys, grad_values)
    )
    query_low = query_part.astype(jnp.bfloat16)
    key_low = key_part.astype(jnp.bfloat16)
    value_low = value_part.astype(jnp.bfloat16)
    query_weight_grad = matmul(lowered_normed.T, query_low)
    key_weight_part = lax.dynamic_update_slice_in_dim(
        jnp.zeros(key_matrix.shape, jnp.float32),
        matmul(lowered_normed.T, key_low),
        key_value_index * head_number,
        1,
    )
    value_weight_part = lax.dynamic_update_slice_in_dim(
        jnp.zeros(value_matrix.shape, jnp.float32),
        matmul(lowered_normed.T, value_low),
        key_value_index * head_number,
        1,
    )
    grad_normed_heads = lax.psum(
        (
            matmul(query_low, query_weight.T)
            + matmul(key_low, key_slice.T)
            + matmul(value_low, value_slice.T)
        ).astype(jnp.bfloat16),
        "tensor",
    ).astype(jnp.float32)
    grad_outer_low = grad_outer.astype(jnp.bfloat16)
    laurel_right_grad = matmul(laurel_inner.T, grad_outer_low)
    grad_inner_low = matmul(grad_outer_low, laurel_right.T).astype(jnp.bfloat16)
    laurel_left_grad = matmul(lowered_normed.T, grad_inner_low)
    grad_normed = grad_normed_heads + grad_normed_mix + matmul(grad_inner_low, laurel_left.T)
    grad_source_norm, input_gain_grad = input_pull(grad_normed)
    residual_grad = (grad_source + grad_source_norm).astype(jnp.bfloat16)
    key_weight_grad, value_weight_grad, query_gain_grad, key_gain_grad = (
        lax.psum_scatter(key_weight_part, ("dp", "tensor"), scatter_dimension=0, tiled=True),
        lax.psum_scatter(value_weight_part, ("dp", "tensor"), scatter_dimension=0, tiled=True),
        lax.psum_scatter(query_gain_part, ("dp", "tensor"), scatter_dimension=0, tiled=True),
        lax.psum_scatter(key_gain_part, ("dp", "tensor"), scatter_dimension=0, tiled=True),
    )
    all_sums = (
        lax.psum_scatter(
            gate_weight_grad.astype(jnp.bfloat16), "dp", scatter_dimension=0, tiled=True
        ).astype(jnp.float32),
        lax.psum_scatter(
            up_weight_grad.astype(jnp.bfloat16), "dp", scatter_dimension=0, tiled=True
        ).astype(jnp.float32),
        lax.psum_scatter(
            down_weight_grad.astype(jnp.bfloat16), "dp", scatter_dimension=1, tiled=True
        ).astype(jnp.float32),
        lax.psum_scatter(
            layer_gate_grad.astype(jnp.bfloat16), "dp", scatter_dimension=0, tiled=True
        ).astype(jnp.float32),
        lax.psum_scatter(
            layer_project_grad.astype(jnp.bfloat16), "dp", scatter_dimension=1, tiled=True
        ).astype(jnp.float32),
        lax.psum_scatter(
            geglu_gain_grad.astype(jnp.bfloat16), "dp", scatter_dimension=0, tiled=True
        ).astype(jnp.float32),
        lax.psum_scatter(
            output_gain_grad.astype(jnp.bfloat16), "dp", scatter_dimension=0, tiled=True
        ).astype(jnp.float32),
        lax.psum_scatter(
            layer_gain_grad.astype(jnp.bfloat16), "dp", scatter_dimension=0, tiled=True
        ).astype(jnp.float32),
        lax.psum_scatter(
            query_weight_grad.astype(jnp.bfloat16), "dp", scatter_dimension=0, tiled=True
        ).astype(jnp.float32),
        lax.psum_scatter(
            mixer_weight_grad.astype(jnp.bfloat16), "dp", scatter_dimension=1, tiled=True
        ).astype(jnp.float32),
        lax.psum_scatter(
            laurel_left_grad.astype(jnp.bfloat16), "dp", scatter_dimension=0, tiled=True
        ).astype(jnp.float32),
        lax.psum_scatter(
            laurel_right_grad.astype(jnp.bfloat16), "dp", scatter_dimension=1, tiled=True
        ).astype(jnp.float32),
        lax.psum_scatter(
            input_gain_grad.astype(jnp.bfloat16), "dp", scatter_dimension=0, tiled=True
        ).astype(jnp.float32),
        lax.psum_scatter(
            laurel_gain_grad.astype(jnp.bfloat16), "dp", scatter_dimension=0, tiled=True
        ).astype(jnp.float32),
        lax.psum_scatter(
            mixer_gain_grad.astype(jnp.bfloat16), "dp", scatter_dimension=0, tiled=True
        ).astype(jnp.float32),
    )
    (
        gate_sum,
        up_sum,
        down_sum,
        layer_gate_sum,
        layer_project_sum,
        geglu_sum,
        output_sum,
        layer_sum,
    ) = all_sums[:8]
    query_sum, mixer_sum, left_sum, right_sum, input_sum, laurel_sum, mixer_gain_sum = all_sums[8:]
    return (
        output,
        residual_grad,
        layer_inputs_grad,
        input_sum,
        left_sum,
        right_sum,
        laurel_sum,
        query_sum,
        key_weight_grad,
        value_weight_grad,
        query_gain_grad,
        key_gain_grad,
        mixer_sum,
        mixer_gain_sum,
        geglu_sum,
        gate_sum,
        up_sum,
        down_sum,
        output_sum,
        layer_gate_sum,
        layer_project_sum,
        layer_sum,
    )


def solution(mesh):
    return jax.shard_map(
        on_device,
        mesh=mesh,
        in_specs=(
            P("dp", None),
            P("dp", None),
            P("dp"),
            P("dp", None),
            P(),
            P(),
            P(),
            P(),
            P(None, "tensor"),
            P(),
            P(),
            P(),
            P(),
            P("tensor", None),
            P(),
            P(),
            P(None, "tensor"),
            P(None, "tensor"),
            P("tensor", None),
            P(),
            P(),
            P(),
            P(),
        ),
        out_specs=(
            P("dp", None),
            P("dp", None),
            P("dp", None),
            P("dp"),
            P("dp", None),
            P(None, "dp"),
            P("dp"),
            P("dp", "tensor"),
            P(("dp", "tensor"), None),
            P(("dp", "tensor"), None),
            P(("dp", "tensor")),
            P(("dp", "tensor")),
            P("tensor", "dp"),
            P("dp"),
            P("dp"),
            P("dp", "tensor"),
            P("dp", "tensor"),
            P("tensor", "dp"),
            P("dp"),
            P("dp", None),
            P(None, "dp"),
            P("dp"),
        ),
        check_vma=False,
    )
```

profile of v0, /device:TPU:0, one launch (start us, length us, event | category | flops | bytes accessed | tf_op | source)
XLA Modules:
  0.0 1748.7 jit_solution(14856395370374370248)
XLA Ops:
  31.3 7.5 multiply_reduce_fusion.7
  58.6 15.6 all-gather.6.cloned.1.call-done
  79.6 42.5 %all-gather.4.cloned.1.call-done = bf16[8192,256]{1,0:T(8,128)(2,1)} async-done(((bf16[1024,256]{1,0:T(8,128)(2,1)}), bf16[8192,256]{1,0:T(8,128)(2,1)}) %all-gather.4.cloned.1.call-update) | async-done | bytes 4194320 | tf_op jit(solution)/shard_map/all_gather | solution.py:150
  122.1 5.9 while.2
  142.5 5.4 multiply_reduce_fusion.4
  148.0 109.2 %all-reduce.21.cloned.1.call-done = bf16[1280,2048]{1,0:T(8,128)(2,1)} async-done(((bf16[1280,2048]{1,0:T(8,128)(2,1)}), bf16[1280,2048]{1,0:T(8,128)(2,1)}) %all-reduce.21.cloned.1.call-update) | async-done | bytes 5242896 | tf_op jit(solution)/shard_map/psum | solution.py:181
  261.6 9.6 multiply_reduce_fusion.3
  276.7 17.3 fusion.150
  294.0 20.7 %multiply_convert_fusion.1 = (bf16[1280,2048]{1,0:T(8,128)(2,1)S(1)}, f32[1280,2048]{1,0:T(8,128)}) fusion(f32[1280,2048]{1,0:T(8,128)} %fusion.150, bf16[1280,2048]{1,0:T(8,128)(2,1)} %multiply_convert_fusion.2, bf16[2048,2048]{1,0:T(8,128)(2,1)} %param.40), kind=kOutput, calls=%fused_computation.80 | convolution fusion | flops 10763632640 | bytes 39845888 | tf_op jit(solution)/shard_map/dot_general | solution.py:23
  317.0 15.0 convolution_convert_fusion.4
  332.1 121.0 %all-reduce.23.cloned.1.call-done = bf16[1280,2048]{1,0:T(8,128)(2,1)} async-done(((bf16[1280,2048]{1,0:T(8,128)(2,1)}), bf16[1280,2048]{1,0:T(8,128)(2,1)}) %all-reduce.23.cloned.1.call-update) | async-done | bytes 5242896 | tf_op jit(solution)/shard_map/psum | solution.py:199
  456.7 10.8 fusion.46
  472.1 6.6 multiply_reduce_fusion.2
  478.7 9.5 fusion.27
  488.3 13.0 fusion.28
  504.8 7.6 fusion.15
  512.4 5.5 fusion.29
  518.0 29.2 %multiply_convert_fusion = (bf16[1280,2048]{1,0:T(8,128)(2,1)}, bf16[1280,2048]{1,0:T(8,128)(2,1)}) fusion(f32[1280,2048]{1,0:T(8,128)} %fusion.150, f32[1280,2048]{1,0:T(8,128)} %get-tuple-element.142, bf16[1280,2048]{1,0:T(8,128)(2,1)} %fusion.29, bf16[2048,2048]{1,0:T(8,128)(2,1)} %param.41), kind=kOutput, calls=%fused_computation.77 | convolution fusion | flops 10800332800 | bytes 45088768 | tf_op jit(solution)/shard_map/dot_general | solution.py:23
  547.1 15.2 fusion.152
  562.4 16.6 add_convert_fusion.1
  581.7 118.5 %all-reduce.25.cloned.1.call-done = bf16[1280,2048]{1,0:T(8,128)(2,1)} async-done(((bf16[1280,2048]{1,0:T(8,128)(2,1)}), bf16[1280,2048]{1,0:T(8,128)(2,1)}) %all-reduce.25.cloned.1.call-update) | async-done | bytes 5242896 | tf_op jit(solution)/shard_map/psum | solution.py:228
  700.1 9.7 fusion.19
  709.9 19.0 %fusion.16 = (bf16[2048]{0:T(1024)(128)(2,1)}, f32[1280]{0:T(1024)S(1)}, f32[1280]{0:T(1024)S(1)}, bf16[2048]{0:T(1024)(128)(2,1)}, f32[1280,2048]{1,0:T(8,128)S(1)}) fusion(bf16[1280,2048]{1,0:T(8,128)(2,1)} %all-reduce.21.cloned.1.call-done, f32[1280]{0:T(1024)S(1)} %copy-done.79, f32[2048]{0:T(1024)S(1)} %broadcast_multiply_fusion.1, ...), kind=kLoop, calls=%fused_computation.47 | loop fusion | flops 55043584 | bytes 52492288 | tf_op jit(solution)/shard_map/transpose(jvp())/reduce_sum | solution.py:19
  729.0 12.0 fusion.32
  789.0 7.1 convolution_convert_fusion.5
  796.5 5.7 fusion.41
  813.0 7.1 convolution_convert_fusion.6
  820.6 16.8 convolution_convert_fusion.1
  837.5 16.8 convolution_convert_fusion.3
  854.3 16.8 convolution_convert_fusion.2
  873.2 5.4 fusion.153
  896.1 8.7 add_convert_fusion
  907.4 5.5 convolution_dynamic-update-slice_fusion
  915.6 5.5 convolution_dynamic-update-slice_fusion.1
  925.7 27.1 %reduce-scatter.18.cloned.1.call-done = bf16[256,64]{0,1:T(8,128)(2,1)} async-done(((bf16[2048,64]{0,1:T(8,128)(2,1)}), bf16[256,64]{0,1:T(8,128)(2,1)}) %reduce-scatter.18.cloned.1.call-update) | async-done | bytes 32784 | tf_op jit(solution)/shard_map/reduce_scatter | solution.py:368
  954.2 29.8 %reduce-scatter.20.cloned.1.call-done = bf16[64,256]{1,0:T(8,128)(2,1)} async-done(((bf16[64,2048]{1,0:T(8,128)(2,1)}), bf16[64,256]{1,0:T(8,128)(2,1)}) %reduce-scatter.20.cloned.1.call-update) | async-done | bytes 32784 | tf_op jit(solution)/shard_map/reduce_scatter | solution.py:371
  985.4 35.6 %reduce-scatter.28.cloned.1.call-done = bf16[512,256]{1,0:T(8,128)(2,1)} async-done(((bf16[512,2048]{1,0:T(8,128)(2,1)}), bf16[512,256]{1,0:T(8,128)(2,1)}) %reduce-scatter.28.cloned.1.call-update) | async-done | bytes 262160 | tf_op jit(solution)/shard_map/reduce_scatter | solution.py:365
  1022.8 35.8 %reduce-scatter.22.cloned.1.call-done = bf16[256,512]{1,0:T(8,128)(2,1)} async-done(((bf16[2048,512]{1,0:T(8,128)(2,1)}), bf16[256,512]{1,0:T(8,128)(2,1)}) %reduce-scatter.22.cloned.1.call-update) | async-done | bytes 262160 | tf_op jit(solution)/shard_map/reduce_scatter | solution.py:362
  1060.4 39.2 %all-reduce.14 = (f32[256]{0:T(256)S(1)}, f32[256]{0:T(256)S(1)}) all-reduce(f32[256]{0:T(256)S(1)} %get-tuple-element.76, f32[256]{0:T(256)S(1)} %get-tuple-element.78), channel_id=12, replica_groups=mesh['dp'=8,'tensor'=4] {'dp','tensor'}, use_global_device_ids=true, to_apply=%region_40.41.clone | all-reduce | flops 512 | bytes 4096
  1100.8 49.1 %reduce-scatter.34.cloned.1.call-done = bf16[2048,256]{1,0:T(8,128)(2,1)} async-done(((bf16[2048,2048]{1,0:T(8,128)(2,1)}), bf16[2048,256]{1,0:T(8,128)(2,1)}) %reduce-scatter.34.cloned.1.call-update) | async-done | bytes 1048592 | tf_op jit(solution)/shard_map/reduce_scatter | solution.py:344
  1152.6 87.4 %reduce-scatter.30.cloned.1.call-done = bf16[256,2048]{1,0:T(8,128)(2,1)} async-done(((bf16[2048,2048]{1,0:T(8,128)(2,1)}), bf16[256,2048]{1,0:T(8,128)(2,1)}) %reduce-scatter.30.cloned.1.call-update) | async-done | bytes 1048592 | tf_op jit(solution)/shard_map/reduce_scatter | solution.py:338
  1242.8 87.4 %reduce-scatter.32.cloned.1.call-done = bf16[256,2048]{1,0:T(8,128)(2,1)} async-done(((bf16[2048,2048]{1,0:T(8,128)(2,1)}), bf16[256,2048]{1,0:T(8,128)(2,1)}) %reduce-scatter.32.cloned.1.call-update) | async-done | bytes 1048592 | tf_op jit(solution)/shard_map/reduce_scatter | solution.py:341
  1333.1 119.7 %all-reduce.27.cloned.1.call-done = bf16[1280,2048]{1,0:T(8,128)(2,1)} async-done(((bf16[1280,2048]{1,0:T(8,128)(2,1)}), bf16[1280,2048]{1,0:T(8,128)(2,1)}) %all-reduce.27.cloned.1.call-update) | async-done | bytes 5242896 | tf_op jit(solution)/shard_map/psum | solution.py:316
  1452.8 11.6 fusion.13
  1464.4 29.1 %all-reduce.15 = (bf16[2048]{0:T(1024)(128)(2,1)S(1)}, bf16[2048]{0:T(1024)(128)(2,1)S(1)}, bf16[2048]{0:T(1024)(128)(2,1)S(1)}, bf16[2048]{0:T(1024)(128)(2,1)S...) all-reduce(bf16[2048]{0:T(1024)(128)(2,1)S(1)} %get-tuple-element.7, ...), channel_id=5, replica_groups=mesh['dp'=8,'tensor'=4] {'dp'}, use_global_device_ids=true, to_apply=%region_31.32.clone | all-reduce | flops 12288 | bytes 49152
  1497.3 12.4 fusion.34
  1509.7 88.9 %reduce-scatter.26.cloned.1.call-done = f32[64,512]{1,0:T(8,128)} async-done(((f32[2048,512]{1,0:T(8,128)}), f32[64,512]{1,0:T(8,128)}) %reduce-scatter.26.cloned.1.call-update) | async-done | bytes 131088 | tf_op jit(solution)/shard_map/reduce_scatter | solution.py:333
  1598.6 143.4 %reduce-scatter.24.cloned.1.call-done = f32[64,512]{1,0:T(8,128)} async-done(((f32[2048,512]{1,0:T(8,128)}), f32[64,512]{1,0:T(8,128)}) %reduce-scatter.24.cloned.1.call-update) | async-done | bytes 131088 | tf_op jit(solution)/shard_map/reduce_scatter | solution.py:332
  (492 shorter events, 206.3 us)
Async XLA Ops:
  7.2 24.1 %copy-start = (bf16[2048,512]{1,0:T(8,128)(2,1)S(1)}, bf16[2048,512]{1,0:T(8,128)(2,1)}, u32[]{:S(2)}) copy-start(bf16[2048,512]{1,0:T(8,128)(2,1)} %param.31) | copy-start | bytes 6291460
  7.2 67.0 %all-gather.6.cloned.1.call-start = ((), (), s32[]{:S(2)}) async-start(), calls=%async_computation.31 | async-start | bytes 4718592 | tf_op jit(solution)/shard_map/all_gather | solution.py:149
  11.1 250.5 %copy-start.68 = (f32[1280]{0:T(1024)}, f32[1280]{0:T(1024)S(1)}, u32[]{:S(2)}) copy-start(f32[1280]{0:T(1024)S(1)} %fusion.118) | copy-start | bytes 15364
  19.6 25.1 %copy-start.74 = (f32[1280]{0:T(1024)}, f32[1280]{0:T(1024)S(1)}, u32[]{:S(2)}) copy-start(f32[1280]{0:T(1024)S(1)} %add_convert_fusion.4) | copy-start | bytes 15364
  24.5 97.6 %all-gather.4.cloned.1.call-start = ((), (), s32[]{:S(2)}) async-start(), calls=%async_computation.13 | async-start | bytes 4718592 | tf_op jit(solution)/shard_map/all_gather | solution.py:150
  31.2 226.0 %all-reduce.21.cloned.1.call-start = ((), (), s32[]{:S(2)}) async-start(), calls=%async_computation.14 | async-start | bytes 10485760 | tf_op jit(solution)/shard_map/psum | solution.py:181
  43.2 87.1 %copy-start.64 = (bf16[2,128,256]{1,2,0:T(8,128)(2,1)}, bf16[2,128,256]{1,2,0:T(8,128)(2,1)S(1)}, u32[]{:S(2)}) copy-start(bf16[2,128,256]{1,2,0:T(8,128)(2,1)S(1)} %copy.104) | copy-start | bytes 393220
  50.2 77.9 %copy-start.58 = (bf16[256,2,256]{2,0,1:T(8,128)(2,1)}, bf16[256,2,256]{2,0,1:T(8,128)(2,1)S(1)}, u32[]{:S(2)}) copy-start(bf16[256,2,256]{2,0,1:T(8,128)(2,1)S(1)} %pad_maximum_fusion.5) | copy-start | bytes 786436
  137.3 315.8 %all-reduce.23.cloned.1.call-start = ((), (), s32[]{:S(2)}) async-start(), calls=%async_computation.15 | async-start | bytes 10485760 | tf_op jit(solution)/shard_map/psum | solution.py:199
  147.9 123.3 %copy-start.84 = (f32[1280]{0:T(1024)}, f32[1280]{0:T(1024)S(1)}, u32[]{:S(2)}) copy-start(f32[1280]{0:T(1024)S(1)} %get-tuple-element.129) | copy-start | bytes 15364
  147.9 113.6 %copy-start.82 = (f32[2048]{0:T(1024)S(1)}, f32[2048]{0:T(1024)}, u32[]{:S(2)}) copy-start(f32[2048]{0:T(1024)} %param.27) | copy-start | bytes 24580
  147.9 113.6 %copy-start.103 = (f32[2048]{0:T(1024)S(1)}, f32[2048]{0:T(1024)}, u32[]{:S(2)}) copy-start(f32[2048]{0:T(1024)} %param.30) | copy-start | bytes 24580
  147.9 113.6 %copy-start.105 = (f32[2048]{0:T(1024)S(1)}, f32[2048]{0:T(1024)}, u32[]{:S(2)}) copy-start(f32[2048]{0:T(1024)} %param.37) | copy-start | bytes 24580
  148.0 123.3 %copy-start.76 = (f32[1280]{0:T(1024)}, f32[1280]{0:T(1024)S(1)}, u32[]{:S(2)}) copy-start(f32[1280]{0:T(1024)S(1)} %fusion.122) | copy-start | bytes 15364
  332.1 124.7 %copy-start.86 = (f32[2048]{0:T(1024)S(1)}, f32[2048]{0:T(1024)}, u32[]{:S(2)}) copy-start(f32[2048]{0:T(1024)} %param.42) | copy-start | bytes 24580
  332.1 368.0 %all-reduce.25.cloned.1.call-start = ((), (), s32[]{:S(2)}) async-start(), calls=%async_computation.16 | async-start | bytes 10485760 | tf_op jit(solution)/shard_map/psum | solution.py:228
  579.0 121.1 %copy-start.88 = (f32[2048]{0:T(1024)S(1)}, f32[2048]{0:T(1024)}, u32[]{:S(2)}) copy-start(f32[2048]{0:T(1024)} %param.38) | copy-start | bytes 24580
  579.0 121.1 %copy-start.90 = (f32[1280]{0:T(1024)S(1)}, f32[1280]{0:T(1024)}, u32[]{:S(2)}) copy-start(f32[1280]{0:T(1024)} %copy-done.89) | copy-start | bytes 15364
  579.1 299.5 %reduce-scatter.16.cloned.1.call-start = ((), (), s32[]{:S(2)}) async-start(), calls=%async_computation.18 | async-start | bytes 4718592 | tf_op jit(solution)/shard_map/reduce_scatter | solution.py:284
  581.6 128.2 %copy-start.94 = (f32[1280]{0:T(1024)S(1)}, f32[1280]{0:T(1024)}, u32[]{:S(2)}) copy-start(f32[1280]{0:T(1024)} %copy-done.93) | copy-start | bytes 15364
  581.6 128.2 %copy-start.77 = (f32[1280]{0:T(1024)S(1)}, f32[1280]{0:T(1024)}, u32[]{:S(2)}) copy-start(f32[1280]{0:T(1024)} %copy-done.76) | copy-start | bytes 15364
  581.6 128.2 %copy-start.79 = (f32[1280]{0:T(1024)S(1)}, f32[1280]{0:T(1024)}, u32[]{:S(2)}) copy-start(f32[1280]{0:T(1024)} %copy-done.78) | copy-start | bytes 15364
  581.6 128.2 %copy-start.102 = (f32[1280]{0:T(1024)S(1)}, f32[1280]{0:T(1024)}, u32[]{:S(2)}) copy-start(f32[1280]{0:T(1024)} %get-tuple-element.125) | copy-start | bytes 15364
  709.8 19.1 %slice-start.3 = ((s8[10485760]{0:T(1024)(128)(4,1)}), s8[4194304]{0:T(1024)(128)(4,1)S(1)}, s32[]{:S(2)}) async-start(s8[10485760]{0:T(1024)(128)(4,1)} %bitcast.229), calls=%async_computation.35 | async-start | bytes 8388608
  709.9 19.1 %slice-start.4 = ((s8[10485760]{0:T(1024)(128)(4,1)}), s8[4194304]{0:T(1024)(128)(4,1)S(1)}, s32[]{:S(2)}) async-start(s8[10485760]{0:T(1024)(128)(4,1)} %bitcast.229), calls=%async_computation.36 | async-start | bytes 8388608
  753.9 131.2 %reduce-scatter.14.cloned.1.call-start = ((), (), s32[]{:S(2)}) async-start(), calls=%async_computation.17 | async-start | bytes 4718592 | tf_op jit(solution)/shard_map/reduce_scatter | solution.py:281
  761.6 160.8 %reduce-scatter.36.cloned.1.call-start = ((), (), s32[]{:S(2)}) async-start(), calls=%async_computation.29 | async-start | bytes 1179648 | tf_op jit(solution)/shard_map/reduce_scatter | solution.py:347
  767.4 156.7 %reduce-scatter.38.cloned.1.call-start = ((), (), s32[]{:S(2)}) async-start(), calls=%async_computation.30 | async-start | bytes 1179648 | tf_op jit(solution)/shard_map/reduce_scatter | solution.py:350
  772.9 180.0 %reduce-scatter.18.cloned.1.call-start = ((), (), s32[]{:S(2)}) async-start(), calls=%async_computation.20 | async-start | bytes 294912 | tf_op jit(solution)/shard_map/reduce_scatter | solution.py:368
  782.3 201.8 %reduce-scatter.20.cloned.1.call-start = ((), (), s32[]{:S(2)}) async-start(), calls=%async_computation.21 | async-start | bytes 294912 | tf_op jit(solution)/shard_map/reduce_scatter | solution.py:371
  788.9 232.1 %reduce-scatter.28.cloned.1.call-start = ((), (), s32[]{:S(2)}) async-start(), calls=%async_computation.25 | async-start | bytes 2359296 | tf_op jit(solution)/shard_map/reduce_scatter | solution.py:365
  796.2 262.4 %reduce-scatter.22.cloned.1.call-start = ((), (), s32[]{:S(2)}) async-start(), calls=%async_computation.22 | async-start | bytes 2359296 | tf_op jit(solution)/shard_map/reduce_scatter | solution.py:362
  820.1 329.8 %reduce-scatter.34.cloned.1.call-start = ((), (), s32[]{:S(2)}) async-start(), calls=%async_computation.28 | async-start | bytes 9437184 | tf_op jit(solution)/shard_map/reduce_scatter | solution.py:344
  837.4 402.6 %reduce-scatter.30.cloned.1.call-start = ((), (), s32[]{:S(2)}) async-start(), calls=%async_computation.26 | async-start | bytes 9437184 | tf_op jit(solution)/shard_map/reduce_scatter | solution.py:338
  854.3 475.9 %reduce-scatter.32.cloned.1.call-start = ((), (), s32[]{:S(2)}) async-start(), calls=%async_computation.27 | async-start | bytes 9437184 | tf_op jit(solution)/shard_map/reduce_scatter | solution.py:341
  871.1 581.6 %all-reduce.27.cloned.1.call-start = ((), (), s32[]{:S(2)}) async-start(), calls=%async_computation.19 | async-start | bytes 10485760 | tf_op jit(solution)/shard_map/psum | solution.py:316
  904.9 693.7 %reduce-scatter.26.cloned.1.call-start = ((), (), s32[]{:S(2)}) async-start(), calls=%async_computation.24 | async-start | bytes 4325376 | tf_op jit(solution)/shard_map/reduce_scatter | solution.py:333
  912.9 829.0 %reduce-scatter.24.cloned.1.call-start = ((), (), s32[]{:S(2)}) async-start(), calls=%async_computation.23 | async-start | bytes 4325376 | tf_op jit(solution)/shard_map/reduce_scatter | solution.py:332
  1022.8 430.0 %copy-start.48 = (bf16[1280,64]{0,1:T(8,128)(2,1)S(1)}, bf16[1280,64]{0,1:T(8,128)(2,1)}, u32[]{:S(2)}) copy-start(bf16[1280,64]{0,1:T(8,128)(2,1)} %copy-done.47) | copy-start | bytes 491524
  1022.8 430.0 %copy-start.53 = (bf16[2048,64]{0,1:T(8,128)(2,1)S(1)}, bf16[2048,64]{0,1:T(8,128)(2,1)}, u32[]{:S(2)}) copy-start(bf16[2048,64]{0,1:T(8,128)(2,1)} %param.28) | copy-start | bytes 786436
  1022.8 430.0 %copy-start.69 = (f32[1280]{0:T(1024)S(1)}, f32[1280]{0:T(1024)}, u32[]{:S(2)}) copy-start(f32[1280]{0:T(1024)} %copy-done.68) | copy-start | bytes 15364
  1022.8 430.0 %copy-start.83 = (f32[2048]{0:T(1024)S(1)}, f32[2048]{0:T(1024)}, u32[]{:S(2)}) copy-start(f32[2048]{0:T(1024)} %param.27) | copy-start | bytes 24580
  1333.0 131.3 %copy-start.115 = (bf16[2048]{0:T(1024)(128)(2,1)S(1)}, bf16[2048]{0:T(1024)(128)(2,1)}, u32[]{:S(2)}) copy-start(bf16[2048]{0:T(1024)(128)(2,1)} %get-tuple-element.64) | copy-start | bytes 12292
  1333.0 131.3 %copy-start.116 = (bf16[2048]{0:T(1024)(128)(2,1)S(1)}, bf16[2048]{0:T(1024)(128)(2,1)}, u32[]{:S(2)}) copy-start(bf16[2048]{0:T(1024)(128)(2,1)} %get-tuple-element.68) | copy-start | bytes 12292
  1333.0 131.3 %copy-start.117 = (bf16[2048]{0:T(1024)(128)(2,1)S(1)}, bf16[2048]{0:T(1024)(128)(2,1)}, u32[]{:S(2)}) copy-start(bf16[2048]{0:T(1024)(128)(2,1)} %get-tuple-element.70) | copy-start | bytes 12292
  1333.0 131.4 %copy-start.118 = (bf16[2048]{0:T(1024)(128)(2,1)S(1)}, bf16[2048]{0:T(1024)(128)(2,1)}, u32[]{:S(2)}) copy-start(bf16[2048]{0:T(1024)(128)(2,1)} %get-tuple-element.75) | copy-start | bytes 12292
  1333.0 131.4 %copy-start.130 = (bf16[2048]{0:T(1024)(128)(2,1)S(1)}, bf16[2048]{0:T(1024)(128)(2,1)}, u32[]{:S(2)}) copy-start(bf16[2048]{0:T(1024)(128)(2,1)} %get-tuple-element.66) | copy-start | bytes 12292
  1333.0 164.3 %copy-start.96 = (f32[1280]{0:T(1024)S(1)}, f32[1280]{0:T(1024)}, u32[]{:S(2)}) copy-start(f32[1280]{0:T(1024)} %copy-done.95) | copy-start | bytes 15364
  (124 other events, 637.5 us)
Sparse Core Ops, SparseCore 0:
  24.6 49.5 all-gather.5
  76.4 45.6 all-gather.3
  137.5 119.6 all-reduce.20
  332.2 120.8 all-reduce.22
  579.2 120.8 all-reduce.24
  754.0 49.9 reduce-scatter.15
  806.2 48.3 reduce-scatter.13
  856.9 31.0 reduce-scatter.35
  890.3 30.7 reduce-scatter.37
  923.8 28.9 reduce-scatter.17
  955.1 28.9 reduce-scatter.19
  986.8 34.2 reduce-scatter.27
  1023.9 34.6 reduce-scatter.21
  1060.7 89.1 reduce-scatter.33
  1152.0 87.9 reduce-scatter.29
  1242.2 88.0 reduce-scatter.31
  1333.4 119.3 all-reduce.26
  1455.5 143.0 reduce-scatter.25
  1601.4 140.4 reduce-scatter.23
where the time goes:
time: 1760 us; the launch traced here: 1750 us
  waiting for transfers between devices  1110 us (63%)
  matrix products  327 us (19%)
  other arithmetic  171 us (10%)
  blocking collectives  68.3 us (4%)
  local copies, waits for them, and re-layouts  51.2 us (3%)
  between operations  18.4 us (1%)
    dot_general x33, matrix products, matmul(): return jnp.dot(left, right, preferred_element_type=jnp.float32)  297 us
    reduce_scatter x1, waiting for transfers between devices, on_device(): lax.psum_scatter(key_weight_part, ('dp', 'tensor'), scatter_dimension=0,...  143 us
    psum x1, waiting for transfers between devices, on_device(): lax.psum(matmul(activation, down_weight).astype(jnp.bfloat16), 'tensor')  121 us
    psum x1, waiting for transfers between devices, on_device(): lax.psum((matmul(query_low, query_weight.T) + matmul(key_low, key_slice.T...  120 us
    psum x1, waiting for transfers between devices, on_device(): lax.psum((matmul(grad_gate_low2, gate_weight.T) + matmul(grad_upper_low,...  118 us
    psum x1, waiting for transfers between devices, on_device(): lax.psum(matmul(mixed_low, mixer_weight).astype(jnp.bfloat16), 'tensor')  109 us
    reduce_scatter x1, waiting for transfers between devices, on_device(): lax.psum_scatter(value_weight_part, ('dp', 'tensor'), scatter_dimension=0...  88.9 us
    reduce_scatter x1, waiting for transfers between devices, on_device(): lax.psum_scatter(gate_weight_grad.astype(jnp.bfloat16), 'dp', scatter_dim...  87.4 us
  transfers between devices with their start and end apart: 19, of which 15 were waited for; matrix products, arithmetic and copies ran while one was open for 14% of the time, Pallas kernels for 0%

commit v1 on v0

v1 whole, which is shorter than its diff:
```python
from functools import partial

import jax
import jax.numpy as jnp
from jax import lax
from jax.sharding import PartitionSpec as P

QUERY_HEADS = 8
KEY_VALUE_HEADS = 2
P_SIZE = 1024
L = 128
CONT_DEV = 2


EPS = 1e-06
THETA = 1000000.0
INV_ROOT = 0.7071067811865476


def rms_norm(value, gain):
    return value * lax.rsqrt(jnp.mean(value * value, axis=-1, keepdims=True) + EPS) * gain


def matmul(left, right):
    return jnp.dot(left, right, preferred_element_type=jnp.float32)


def apply_rotary(values, positions):
    width = values.shape[-1]
    half = width // 2
    freqs = THETA ** (-(jnp.arange(half, dtype=jnp.float32) * 2.0 / width))
    angles = positions.astype(jnp.float32)[:, None] * freqs[None, :]
    cosine = jnp.cos(angles)[:, None, :]
    sine = jnp.sin(angles)[:, None, :]
    first = values[..., :half]
    second = values[..., half:]
    return jnp.concatenate(
        [first * cosine - second * sine, second * cosine + first * sine], axis=-1
    )


def block_positions():
    prompt_part = jnp.arange(P_SIZE, dtype=jnp.int32)
    tail_part = jnp.tile(P_SIZE + jnp.arange(L, dtype=jnp.int32), CONT_DEV)
    return jnp.concatenate([prompt_part, tail_part])


def geglu(gate, other):
    return jax.nn.gelu(gate, approximate=True) * other


def add_norm(base, branch, gain):
    return base + rms_norm(branch, gain)


def masked_scores(queries, keys, allowed):
    scale = queries.shape[-1] ** (-0.5)
    scores = jnp.einsum("qhd,kd->hqk", queries, keys, preferred_element_type=jnp.float32) * scale
    return jnp.where(allowed[None], scores, -1e30)


def attend_forward(queries, keys, values, allowed):
    scores = masked_scores(queries, keys, allowed)
    top = jnp.max(scores, axis=-1, keepdims=True)
    weights = jnp.exp(scores - top)
    totals = jnp.sum(weights, axis=-1, keepdims=True)
    probs = (weights / totals).astype(jnp.bfloat16)
    mixed = jnp.einsum("hqk,kd->qhd", probs, values, preferred_element_type=jnp.float32)
    return (mixed, top + jnp.log(totals))


def attend_backward(queries, keys, values, allowed, log_totals, grad_mixed):
    scale = queries.shape[-1] ** (-0.5)
    probs = jnp.exp(masked_scores(queries, keys, allowed) - log_totals)
    probs_low = probs.astype(jnp.bfloat16)
    grad_probs = jnp.einsum("qhd,kd->hqk", grad_mixed, values, preferred_element_type=jnp.float32)
    centre = jnp.sum(grad_probs * probs, axis=-1, keepdims=True)
    grad_scores = (probs * (grad_probs - centre)).astype(jnp.bfloat16)
    grad_queries = (
        jnp.einsum("hqk,kd->qhd", grad_scores, keys, preferred_element_type=jnp.float32) * scale
    )
    grad_keys = (
        jnp.einsum("hqk,qhd->kd", grad_scores, queries, preferred_element_type=jnp.float32) * scale
    )
    grad_values = jnp.einsum(
        "hqk,qhd->kd", probs_low, grad_mixed, preferred_element_type=jnp.float32
    )
    return (grad_queries, grad_keys, grad_values)


def hop(value, mask):
    return lax.ppermute(value, "tensor", [(place, place ^ mask) for place in range(4)])


def gather_rows(own, size):
    if size != 4:
        return [lax.all_gather(own, "tensor", axis=0, tiled=True)]
    half = own.shape[0] // 2
    first = hop(own, 1)
    second = hop(own, 2)
    third = jnp.concatenate([hop(first[:half], 2), hop(second[half:], 1)], axis=0)
    return [own, first, second, third]


def scatter_rows(parts, size):
    if size != 4:
        return lax.psum_scatter(parts[0], "tensor", scatter_dimension=0, tiled=True).astype(
            jnp.float32
        )
    half = parts[0].shape[0] // 2
    own, first, second, third = parts

    def wide(value):
        return value.astype(jnp.float32)

    def narrow(value):
        return value.astype(jnp.bfloat16)

    far_top = hop(third[:half], 1)
    far_bottom = hop(third[half:], 2)
    near_top = hop(first[:half], 1)
    near_bottom = hop(second[half:], 2)
    onward_top = narrow(wide(second[:half]) + wide(far_top))
    onward_bottom = narrow(wide(first[half:]) + wide(far_bottom))
    last_top = hop(onward_top, 2)
    last_bottom = hop(onward_bottom, 1)
    top = wide(own[:half]) + wide(near_top) + wide(last_top)
    bottom = wide(own[half:]) + wide(near_bottom) + wide(last_bottom)
    return jnp.concatenate([top, bottom], axis=0)


def split_rows(value, place, size):
    if size != 4:
        return [value]
    rows = value.shape[0] // 4
    return [
        lax.dynamic_slice_in_dim(value, jnp.bitwise_xor(place, index) * rows, rows, 0)
        for index in range(4)
    ]


def join_rows(parts, place, size):
    if size != 4:
        return parts[0]
    rows = parts[0].shape[0]
    whole = jnp.zeros((rows * 4,) + parts[0].shape[1:], parts[0].dtype)
    for index in range(4):
        whole = lax.dynamic_update_slice_in_dim(
            whole, parts[index], jnp.bitwise_xor(place, index) * rows, 0
        )
    return whole


def stack_rows(parts):
    return parts[0] if len(parts) == 1 else jnp.concatenate(parts, axis=0)


def narrow(value):
    return value.astype(jnp.bfloat16)


def scatter_sum(value, dimension):
    return lax.psum_scatter(
        narrow(value), "dp", scatter_dimension=dimension, tiled=True
    ).astype(jnp.float32)


def sum_places(value, size):
    if size != 4:
        return lax.psum(value, "tensor")
    value = value + hop(value, 1)
    return value + hop(value, 2)


def on_device(
    mesh_sizes,
    residual_in,
    layer_inputs,
    group_ids,
    cotangent,
    input_gain,
    laurel_left,
    laurel_right,
    laurel_gain,
    query_weight,
    key_matrix,
    value_matrix,
    query_gain,
    key_gain,
    mixer_weight,
    mixer_gain,
    geglu_gain,
    gate_weight,
    up_weight,
    down_weight,
    output_gain,
    layer_gate,
    layer_project,
    layer_gain,
):
    size = mesh_sizes["tensor"]
    blocks = mesh_sizes["dp"]
    place = lax.axis_index("tensor")
    rows = residual_in.shape[0]
    part_rows = rows // size
    width = residual_in.shape[1]
    head_number = query_gain.shape[0]
    device_heads = query_weight.shape[1] // head_number
    conts = group_ids.shape[0]
    key_value_index = place * device_heads // (QUERY_HEADS // KEY_VALUE_HEADS)
    positions = block_positions()

    def own_rows(value):
        return lax.dynamic_slice_in_dim(value, place * part_rows, part_rows, 0)

    lowered_normed = narrow(rms_norm(residual_in.astype(jnp.float32), input_gain))
    residual = own_rows(residual_in).astype(jnp.float32)
    extra = own_rows(layer_inputs).astype(jnp.float32)
    cotangent_own = own_rows(cotangent).astype(jnp.float32)
    normed, input_pull = jax.vjp(rms_norm, residual, input_gain)
    normed_own = narrow(normed)
    key_slice = lax.dynamic_slice_in_dim(key_matrix, key_value_index * head_number, head_number, 1)
    value_slice = lax.dynamic_slice_in_dim(
        value_matrix, key_value_index * head_number, head_number, 1
    )
    unrotated_keys = matmul(lowered_normed, key_slice)
    unrotated_values = matmul(lowered_normed, value_slice)
    queries_raw = matmul(lowered_normed, query_weight)

    def shape_keys(key_part, value_part, gain_key):
        shaped_keys = apply_rotary(rms_norm(key_part, gain_key)[:, None, :], positions)[:, 0]
        return (shaped_keys, rms_norm(value_part, 1.0))

    def shape_queries(query_part, gain_query):
        return apply_rotary(
            rms_norm(query_part.reshape(rows, device_heads, head_number), gain_query), positions
        )

    shaped_keys, keys_pull = jax.vjp(shape_keys, unrotated_keys, unrotated_values, key_gain)
    shaped_queries, queries_pull = jax.vjp(shape_queries, queries_raw, query_gain)
    queries_low = narrow(shaped_queries)
    keys_low = narrow(shaped_keys[0])
    values_low = narrow(shaped_keys[1])
    prompt_both = lax.all_gather(
        jnp.concatenate([keys_low[:P_SIZE], values_low[:P_SIZE]], axis=1), "dp", axis=0, tiled=True
    )
    span = prompt_both.shape[0]
    causal_prompt = jnp.arange(P_SIZE)[:, None] >= jnp.arange(P_SIZE)[None, :]
    causal_tail = jnp.arange(L)[:, None] >= jnp.arange(L)[None, :]
    tail_allowed = jnp.concatenate([jnp.ones((L, P_SIZE), dtype=bool), causal_tail], axis=1)
    prompt_mixed, prompt_lse = attend_forward(
        queries_low[:P_SIZE], keys_low[:P_SIZE], values_low[:P_SIZE], causal_prompt
    )

    def own_prompt(whole, group):
        return lax.dynamic_slice_in_dim(whole, group * P_SIZE, P_SIZE, 0)

    own_both = jax.vmap(own_prompt, in_axes=(None, 0))(prompt_both, group_ids)
    own_keys = own_both[:, :, :head_number]
    own_values = own_both[:, :, head_number:]
    tail_keys = jnp.concatenate(
        [own_keys, keys_low[P_SIZE:].reshape(conts, L, head_number)], axis=1
    )
    tail_values = jnp.concatenate(
        [own_values, values_low[P_SIZE:].reshape(conts, L, head_number)], axis=1
    )
    tail_queries = queries_low[P_SIZE:].reshape(conts, L, device_heads, head_number)
    tail_mixed, tail_lse = jax.vmap(attend_forward, in_axes=(0, 0, 0, None))(
        tail_queries, tail_keys, tail_values, tail_allowed
    )
    tail_mixed = tail_mixed.reshape(conts * L, device_heads, head_number)
    mixed_low = narrow(
        jnp.concatenate([prompt_mixed, tail_mixed], axis=0).reshape(
            rows, device_heads * head_number
        )
    )
    mixed_parts = split_rows(mixed_low, place, size)
    attention = scatter_rows(
        [narrow(matmul(piece, mixer_weight)) for piece in mixed_parts], size
    )
    laurel_inner = narrow(matmul(normed_own, laurel_left))
    laurel_outer = matmul(laurel_inner, laurel_right)

    def mix_all(attended, source, normed_in, outer, gain_mixer, gain_laurel):
        return (
            rms_norm(attended, gain_mixer) + source + normed_in + rms_norm(outer, gain_laurel)
        ) * INV_ROOT

    combined, mix_pull = jax.vjp(
        mix_all, attention, residual, normed, laurel_outer, mixer_gain, laurel_gain
    )
    dense_float, pre_pull = jax.vjp(rms_norm, combined, geglu_gain)
    dense_parts = gather_rows(narrow(dense_float), size)
    gate_pulls = []
    activation_parts = []
    down_parts = []
    for piece in dense_parts:
        gate = matmul(piece, gate_weight)
        upper = matmul(piece, up_weight)
        activation_float, pull = jax.vjp(geglu, gate, upper)
        gate_pulls.append(pull)
        activation_parts.append(narrow(activation_float))
        down_parts.append(narrow(matmul(activation_parts[-1], down_weight)))
    down = scatter_rows(down_parts, size)
    carried, dense_pull = jax.vjp(add_norm, combined, down, output_gain)
    carried_low = narrow(carried)
    layer_gate_out = matmul(carried_low, layer_gate)
    layer_float, layer_pull = jax.vjp(geglu, layer_gate_out, extra)
    layer_act = narrow(layer_float)
    layer_out = matmul(layer_act, layer_project)
    result, tail_pull = jax.vjp(add_norm, carried, layer_out, layer_gain)
    output_own = narrow(result)
    grad_carried, grad_layer_out, layer_gain_grad = tail_pull(cotangent_own)
    grad_layer_low = narrow(grad_layer_out)
    grad_layer_act = matmul(grad_layer_low, layer_project.T)
    grad_gate_out, grad_extra = layer_pull(grad_layer_act)
    layer_inputs_grad_own = narrow(grad_extra)
    grad_gate_low = narrow(grad_gate_out)
    grad_carried = grad_carried + matmul(grad_gate_low, layer_gate.T)
    grad_combined, grad_down, output_gain_grad = dense_pull(grad_carried)
    grad_down_parts = gather_rows(narrow(grad_down), size)
    gate_low_parts = []
    upper_low_parts = []
    dense_grad_parts = []
    for piece, pull in zip(grad_down_parts, gate_pulls):
        grad_gate, grad_upper = pull(matmul(piece, down_weight.T))
        gate_low_parts.append(narrow(grad_gate))
        upper_low_parts.append(narrow(grad_upper))
        dense_grad_parts.append(
            narrow(
                matmul(gate_low_parts[-1], gate_weight.T)
                + matmul(upper_low_parts[-1], up_weight.T)
            )
        )
    down_sum = scatter_sum(
        matmul(stack_rows(activation_parts).T, stack_rows(grad_down_parts)), 1
    )
    dense_whole = stack_rows(dense_parts)
    gate_sum = scatter_sum(matmul(dense_whole.T, stack_rows(gate_low_parts)), 0)
    up_sum = scatter_sum(matmul(dense_whole.T, stack_rows(upper_low_parts)), 0)
    grad_dense = scatter_rows(dense_grad_parts, size)
    output_own, grad_dense = lax.optimization_barrier((output_own, grad_dense))
    output = join_rows(gather_rows(output_own, size), place, size)
    layer_inputs_grad = join_rows(gather_rows(layer_inputs_grad_own, size), place, size)
    layer_gate_grad = matmul(carried_low.T, grad_gate_low)
    layer_project_grad = matmul(grad_layer_low.T, layer_act)
    grad_combined_pre, geglu_gain_grad = pre_pull(grad_dense)
    grad_combined = grad_combined + grad_combined_pre
    grad_attention, grad_source, grad_normed_mix, grad_outer, mixer_gain_grad, laurel_gain_grad = (
        mix_pull(grad_combined)
    )
    grad_attention_parts = gather_rows(narrow(grad_attention), size)
    mixer_sum = scatter_sum(
        matmul(stack_rows(mixed_parts).T, stack_rows(grad_attention_parts)), 1
    )
    grad_mixed = join_rows(
        [narrow(matmul(piece, mixer_weight.T)) for piece in grad_attention_parts], place, size
    ).reshape(rows, device_heads, head_number)
    prompt_dq, prompt_dk, prompt_dv = attend_backward(
        queries_low[:P_SIZE],
        keys_low[:P_SIZE],
        values_low[:P_SIZE],
        causal_prompt,
        prompt_lse,
        grad_mixed[:P_SIZE],
    )
    tail_dq, tail_dk, tail_dv = jax.vmap(attend_backward, in_axes=(0, 0, 0, None, 0, 0))(
        tail_queries,
        tail_keys,
        tail_values,
        tail_allowed,
        tail_lse,
        grad_mixed[P_SIZE:].reshape(conts, L, device_heads, head_number),
    )
    cont_both = jnp.concatenate([tail_dk[:, :P_SIZE], tail_dv[:, :P_SIZE]], axis=2)
    spread = jnp.zeros((span, 2 * head_number), jnp.float32)
    for index in range(conts):
        start = group_ids[index] * P_SIZE
        spread = lax.dynamic_update_slice_in_dim(
            spread,
            lax.dynamic_slice_in_dim(spread, start, P_SIZE, 0) + cont_both[index],
            start,
            0,
        )
    owner_both = scatter_sum(spread, 0)
    grad_queries = jnp.concatenate(
        [prompt_dq, tail_dq.reshape(conts * L, device_heads, head_number)], axis=0
    )
    grad_keys = jnp.concatenate(
        [
            prompt_dk + owner_both[:, :head_number],
            tail_dk[:, P_SIZE:].reshape(conts * L, head_number),
        ],
        axis=0,
    )
    grad_values = jnp.concatenate(
        [
            prompt_dv + owner_both[:, head_number:],
            tail_dv[:, P_SIZE:].reshape(conts * L, head_number),
        ],
        axis=0,
    )
    query_part, query_gain_part = queries_pull(grad_queries)
    query_low = narrow(query_part)
    query_sum = scatter_sum(matmul(lowered_normed.T, query_low), 0)
    key_part, value_part, key_gain_part = keys_pull((grad_keys, grad_values))
    both_low = jnp.concatenate([narrow(key_part), narrow(value_part)], axis=1)
    both_weight = jnp.concatenate([key_slice, value_slice], axis=1)
    both_sum = scatter_sum(matmul(lowered_normed.T, both_low), 0)
    grad_normed_heads = scatter_rows(
        [
            narrow(matmul(query_piece, query_weight.T) + matmul(both_piece, both_weight.T))
            for query_piece, both_piece in zip(
                split_rows(query_low, place, size), split_rows(both_low, place, size)
            )
        ],
        size,
    )
    grad_outer_low = narrow(grad_outer)
    laurel_right_grad = matmul(grad_outer_low.T, laurel_inner)
    grad_inner_low = narrow(matmul(grad_outer_low, laurel_right.T))
    laurel_left_grad = matmul(normed_own.T, grad_inner_low)
    grad_normed = grad_normed_heads + grad_normed_mix + matmul(grad_inner_low, laurel_left.T)
    grad_source_norm, input_gain_grad = input_pull(grad_normed)
    residual_grad = join_rows(
        gather_rows(narrow(grad_source + grad_source_norm), size), place, size
    )
    share = width // blocks

    def place_gain(part):
        pieces = part.reshape(blocks, head_number // blocks)
        padded = jnp.pad(pieces, ((0, 0), (0, share - pieces.shape[1])))
        return padded.reshape(width)

    gains = jnp.stack(
        [
            input_gain_grad,
            laurel_gain_grad,
            mixer_gain_grad,
            geglu_gain_grad,
            output_gain_grad,
            layer_gain_grad,
            place_gain(query_gain_part),
            place_gain(key_gain_part),
        ],
        axis=1,
    )
    small = jnp.concatenate(
        [
            narrow(layer_gate_grad),
            narrow(layer_project_grad),
            narrow(laurel_left_grad),
            narrow(laurel_right_grad),
            narrow(gains),
        ],
        axis=1,
    )
    small_sum = sum_places(scatter_sum(small, 0), size)
    inner = laurel_left.shape[1]
    plain = extra.shape[1]
    layer_gate_sum = small_sum[:, :plain]
    layer_project_sum = small_sum[:, plain : 2 * plain].T
    left_sum = small_sum[:, 2 * plain : 2 * plain + inner]
    right_sum = small_sum[:, 2 * plain + inner : 2 * plain + 2 * inner].T
    gain_sums = small_sum[:, 2 * plain + 2 * inner :].T
    input_sum, laurel_sum, mixer_gain_sum, geglu_sum, output_sum, layer_sum = gain_sums[:6]
    gain_piece = head_number // (blocks * size)
    query_gain_grad = lax.dynamic_slice_in_dim(gain_sums[6], place * gain_piece, gain_piece, 0)
    key_gain_grad = lax.dynamic_slice_in_dim(gain_sums[7], place * gain_piece, gain_piece, 0)
    spread_both = lax.dynamic_update_slice_in_dim(
        jnp.zeros((share, KEY_VALUE_HEADS, 2 * head_number), jnp.float32),
        both_sum[:, None, :],
        key_value_index,
        1,
    )
    both_grad = lax.psum_scatter(spread_both, "tensor", scatter_dimension=0, tiled=True)
    key_weight_grad = both_grad[:, :, :head_number].reshape(-1, KEY_VALUE_HEADS * head_number)
    value_weight_grad = both_grad[:, :, head_number:].reshape(-1, KEY_VALUE_HEADS * head_number)
    return (
        output,
        residual_grad,
        layer_inputs_grad,
        input_sum,
        left_sum,
        right_sum,
        laurel_sum,
        query_sum,
        key_weight_grad,
        value_weight_grad,
        query_gain_grad,
        key_gain_grad,
        mixer_sum,
        mixer_gain_sum,
        geglu_sum,
        gate_sum,
        up_sum,
        down_sum,
        output_sum,
        layer_gate_sum,
        layer_project_sum,
        layer_sum,
    )


def solution(mesh):
    return jax.shard_map(
        partial(on_device, dict(mesh.shape)),
        mesh=mesh,
        in_specs=(
            P("dp", None),
            P("dp", None),
            P("dp"),
            P("dp", None),
            P(),
            P(),
            P(),
            P(),
            P(None, "tensor"),
            P(),
            P(),
            P(),
            P(),
            P("tensor", None),
            P(),
            P(),
            P(None, "tensor"),
            P(None, "tensor"),
            P("tensor", None),
            P(),
            P(),
            P(),
            P(),
        ),
        out_specs=(
            P("dp", None),
            P("dp", None),
            P("dp", None),
            P("dp"),
            P("dp", None),
            P(None, "dp"),
            P("dp"),
            P("dp", "tensor"),
            P(("dp", "tensor"), None),
            P(("dp", "tensor"), None),
            P(("dp", "tensor")),
            P(("dp", "tensor")),
            P("tensor", "dp"),
            P("dp"),
            P("dp"),
            P("dp", "tensor"),
            P("dp", "tensor"),
            P("tensor", "dp"),
            P("dp"),
            P("dp", None),
            P(None, "dp"),
            P("dp"),
        ),
        check_vma=False,
    )
```

time: 1760 us -> 1260 us (0.72)
  waiting for transfers between devices: 1110 us -> 578 us
  local copies, waits for them, and re-layouts: 51.2 us -> 172 us
  other arithmetic: 171 us -> 87.8 us
  blocking collectives: 68.3 us -> 0 us
  starting transfers between devices: 2.16 us -> 54.9 us
    psum x4 -> x0, waiting for transfers between devices: 468 us -> none  [the longest x1 121 us: on_device(): lax.psum(matmul(activation, down_weight).astype(jnp.bfloat16), 'tensor')]
    reduce_scatter x13 -> x8, waiting for transfers between devices: 585 us -> 281 us  [scatter_sum(): lax.psum_scatter(narrow(value), 'dp', scatter_dimension=dimension, tiled=...]
    ppermute x0 -> x50, waiting for transfers between devices: none -> 210 us  [hop(): lax.ppermute(value, 'tensor', [(place, place ^ mask) for place in range(4)])]
    unnamed x2 -> x0, blocking collectives: 68.3 us -> none
    convert_element_type x28 -> x22, other arithmetic: 90.5 us -> 28 us  [the longest x7 15.2 us: scatter_sum(): return lax.psum_scatter(narrow(value), 'dp', scatter_dimension=dimension,...]
    ppermute x0 -> x50, starting transfers between devices: none -> 54.3 us  [hop(): lax.ppermute(value, 'tensor', [(place, place ^ mask) for place in range(4)])]
    dynamic_update_slice x2 -> x12, local copies, waits for them, and re-layouts: 0.15 us -> 39.2 us  [the longest x11 30.6 us: join_rows(): lax.dynamic_update_slice_in_dim(whole, parts[index], jnp.bitwise_xor(plac...]
    unnamed x19 -> x11, waiting for transfers between devices: 0.31 us -> 34.3 us
  transfers between devices with their start and end apart: 19 -> 60, of which waited for: 15 -> 32; matrix products, arithmetic and copies ran while one was open for 14% -> 35% of each run, Pallas kernels for 0% -> 0%
where the time goes in v1:
time: 1260 us; the launch traced here: 1250 us
  waiting for transfers between devices  578 us (46%)
  matrix products  335 us (27%)
  local copies, waits for them, and re-layouts  172 us (14%)
  other arithmetic  87.8 us (7%)
  starting transfers between devices  54.9 us (4%)
  between operations  19.2 us (2%)
    dot_general x61, matrix products, matmul(): return jnp.dot(left, right, preferred_element_type=jnp.float32)  315 us
    reduce_scatter x8, waiting for transfers between devices, scatter_sum(): lax.psum_scatter(narrow(value), 'dp', scatter_dimension=dimension, tiled=...  281 us
    ppermute x50, waiting for transfers between devices, hop(): lax.ppermute(value, 'tensor', [(place, place ^ mask) for place in range(4)])  210 us
    ppermute x50, starting transfers between devices, hop(): lax.ppermute(value, 'tensor', [(place, place ^ mask) for place in range(4)])  54.3 us
    all_gather x1, waiting for transfers between devices, on_device(): lax.all_gather(jnp.concatenate([keys_low[:P_SIZE], values_low[:P_SIZE]],...  51.9 us
    unnamed x427, local copies, waits for them, and re-layouts  48.6 us
    unnamed x11, waiting for transfers between devices  34.3 us
    dynamic_update_slice x11, local copies, waits for them, and re-layouts, join_rows(): lax.dynamic_update_slice_in_dim(whole, parts[index], jnp.bitwise_xor(plac...  30.6 us
  transfers between devices with their start and end apart: 60, of which 32 were waited for; matrix products, arithmetic and copies ran while one was open for 35% of the time, Pallas kernels for 0%

profile of v1, /device:TPU:0, one launch (start us, length us, event | category | flops | bytes accessed | tf_op | source)
XLA Modules:
  0.0 1247.1 jit_solution(2455386314053347099)
XLA Ops:
  32.8 7.2 multiply_reduce_fusion.15
  65.6 51.9 %all-gather.2.cloned.1.call-done = bf16[8192,512]{1,0:T(8,128)(2,1)} async-done(((bf16[1024,512]{1,0:T(8,128)(2,1)}), bf16[8192,512]{1,0:T(8,128)(2,1)}) %all-gather.2.cloned.1.call-update) | async-done | bytes 8388624 | tf_op jit(solution)/shard_map/all_gather | solution.py:244
  142.9 10.9 collective-permute-done.4
  158.9 11.1 collective-permute-done
  170.0 13.0 %collective-permute-done.5 = bf16[160,2048]{1,0:T(8,128)(2,1)S(1)} collective-permute-done((bf16[160,2048]{1,0:T(8,128)(2,1)S(1)}, bf16[160,2048]{1,0:T(8,128)(2,1)S(1)}, u32[]{:S(2)}, u32[]{:S(2)}) %collective-permute-start.5) | collective-permute-done | bytes 655392 | tf_op jit(solution)/shard_map/ppermute | solution.py:92
  195.5 9.2 multiply_convert_fusion.7
  204.7 15.6 %collective-permute-done.6 = bf16[320,2048]{1,0:T(8,128)(2,1)S(1)} collective-permute-done((bf16[320,2048]{1,0:T(8,128)(2,1)S(1)}, bf16[320,2048]{1,0:T(8,128)(2,1)S(1)}, u32[]{:S(2)}, u32[]{:S(2)}) %collective-permute-start.6) | collective-permute-done | bytes 1310752 | tf_op jit(solution)/shard_map/ppermute | solution.py:92
  225.6 9.0 multiply_convert_fusion.6
  244.3 9.0 multiply_convert_fusion.5
  253.9 7.6 fusion.253
  261.5 9.0 multiply_convert_fusion.4
  280.5 11.8 collective-permute-done.14
  298.0 8.3 collective-permute-done.13
  306.3 10.2 collective-permute-done.12
  332.5 9.7 multiply_convert_fusion.3
  342.2 8.2 fusion.254
  350.4 7.2 collective-permute-done.16
  361.2 11.7 multiply_convert_fusion.2
  373.0 6.5 fusion.255
  379.5 6.4 fusion.43
  387.7 12.3 multiply_convert_fusion.1
  400.1 8.3 fusion.256
  408.3 12.0 multiply_convert_fusion
  420.4 6.7 fusion.257
  427.1 6.5 fusion.45
  435.4 6.4 fusion.44
  443.4 8.0 collective-permute-done.24
  453.5 6.3 fusion.42
  465.2 7.0 collective-permute-done.22
  485.4 20.0 %collective-permute-done.30 = bf16[320,2048]{1,0:T(8,128)(2,1)} collective-permute-done((bf16[320,2048]{1,0:T(8,128)(2,1)}, bf16[320,2048]{1,0:T(8,128)(2,1)}, u32[]{:S(2)}, u32[]{:S(2)}) %collective-permute-start.30) | collective-permute-done | bytes 1310752 | tf_op jit(solution)/shard_map/ppermute | solution.py:92
  615.0 50.4 %reduce-scatter.9.cloned.1.call-done = bf16[1024,512]{1,0:T(8,128)(2,1)} async-done(((bf16[8192,512]{1,0:T(8,128)(2,1)}), bf16[1024,512]{1,0:T(8,128)(2,1)}) %reduce-scatter.9.cloned.1.call-update) | async-done | bytes 1048592 | tf_op jit(solution)/shard_map/reduce_scatter | solution.py:163
  689.7 9.0 collective-permute-done.38
  701.2 15.1 %collective-permute-done.35 = bf16[160,2048]{1,0:T(8,128)(2,1)S(1)} collective-permute-done((bf16[160,2048]{1,0:T(8,128)(2,1)S(1)}, bf16[160,2048]{1,0:T(8,128)(2,1)S(1)}, u32[]{:S(2)}, u32[]{:S(2)}) %collective-permute-start.35) | collective-permute-done | bytes 655392 | tf_op jit(solution)/shard_map/ppermute | solution.py:92
  734.8 11.0 concatenate.145
  747.0 7.1 convolution_convert_fusion.4
  767.5 6.7 convolution_convert_fusion.3
  774.3 7.6 convolution_convert_fusion.5
  788.0 15.9 %convolution_convert_fusion = bf16[2048,2048]{1,0:T(8,128)(2,1)} fusion(bf16[1280,2048]{1,0:T(8,128)(2,1)} %constant_dynamic-update-slice_fusion.12, bf16[320,2048]{1,0:T(8,128)(2,1)S(1)} %copy-done.195, bf16[320,2048]{1,0:T(8,128)(2,1)S(1)} %copy-done.193, bf16[320,2048]{1,0:T(8,128)(2,1)S(1)} %copy-done.191, bf16[320,2048]{1,0:T(8,128)(2,1)S(1)} %copy-done.189), kind=kOutput, calls=%fused_computation.16 | convolution fusion | flops 10762584064 | bytes 18874368 | tf_op jit(solution)/shard_map/dot_general | solution.py:25
  805.3 16.6 %convolution_convert_fusion.1 = bf16[2048,2048]{1,0:T(8,128)(2,1)} fusion(bf16[1280,2048]{1,0:T(8,128)(2,1)} %copy-done.101, bf16[320,2048]{1,0:T(8,128)(2,1)} %copy-done.183, bf16[320,2048]{1,0:T(8,128)(2,1)} %get-tuple-element.154, bf16[320,2048]{1,0:T(8,128)(2,1)} %copy-done.181, bf16[320,2048]{1,0:T(8,128)(2,1)S(1)} %copy-done.180), kind=kOutput, calls=%fused_computation.17 | convolution fusion | flops 10762584064 | bytes 18874368 | tf_op jit(solution)/shard_map/dot_general | solution.py:25
  823.2 16.5 %convolution_convert_fusion.2 = bf16[2048,2048]{1,0:T(8,128)(2,1)} fusion(bf16[1280,2048]{1,0:T(8,128)(2,1)} %copy-done.101, bf16[320,2048]{1,0:T(8,128)(2,1)} %copy-done.187, bf16[320,2048]{1,0:T(8,128)(2,1)} %copy-done.186, bf16[320,2048]{1,0:T(8,128)(2,1)} %copy-done.185, bf16[320,2048]{1,0:T(8,128)(2,1)S(1)} %copy-done.184), kind=kOutput, calls=%fused_computation.18 | convolution fusion | flops 10762584064 | bytes 18874368 | tf_op jit(solution)/shard_map/dot_general | solution.py:25
  871.4 15.2 %collective-permute-done.26 = bf16[320,2048]{1,0:T(8,128)(2,1)S(1)} collective-permute-done((bf16[320,2048]{1,0:T(8,128)(2,1)S(1)}, bf16[320,2048]{1,0:T(8,128)(2,1)S(1)}, u32[]{:S(2)}, u32[]{:S(2)}) %collective-permute-start.26) | collective-permute-done | bytes 1310752 | tf_op jit(solution)/shard_map/ppermute | solution.py:92
  898.9 8.6 dynamic_update_slice.75
  908.6 15.2 %collective-permute-done.28 = bf16[160,2048]{1,0:T(8,128)(2,1)} collective-permute-done((bf16[160,2048]{1,0:T(8,128)(2,1)}, bf16[160,2048]{1,0:T(8,128)(2,1)}, u32[]{:S(2)}, u32[]{:S(2)}) %collective-permute-start.28) | collective-permute-done | bytes 655392 | tf_op jit(solution)/shard_map/ppermute | solution.py:92
  934.9 55.5 %reduce-scatter.23.cloned.1.call-done = bf16[2048,256]{1,0:T(8,128)(2,1)} async-done(((bf16[2048,2048]{1,0:T(8,128)(2,1)}), bf16[2048,256]{1,0:T(8,128)(2,1)}) %reduce-scatter.23.cloned.1.call-update) | async-done | bytes 1048592 | tf_op jit(solution)/shard_map/reduce_scatter | solution.py:163
  993.1 87.6 %reduce-scatter.21.cloned.1.call-done = bf16[256,2048]{1,0:T(8,128)(2,1)} async-done(((bf16[2048,2048]{1,0:T(8,128)(2,1)}), bf16[256,2048]{1,0:T(8,128)(2,1)}) %reduce-scatter.21.cloned.1.call-update) | async-done | bytes 1048592 | tf_op jit(solution)/shard_map/reduce_scatter | solution.py:163
  1083.5 87.5 %reduce-scatter.19.cloned.1.call-done = bf16[256,2048]{1,0:T(8,128)(2,1)} async-done(((bf16[2048,2048]{1,0:T(8,128)(2,1)}), bf16[256,2048]{1,0:T(8,128)(2,1)}) %reduce-scatter.19.cloned.1.call-update) | async-done | bytes 1048592 | tf_op jit(solution)/shard_map/reduce_scatter | solution.py:163
  1186.0 12.2 collective-permute-done.42
  1199.4 34.1 %all-reduce.11.cloned.1.call-done = f32[256,2,512]{2,1,0:T(2,128)} async-done(((f32[256,2,512]{2,1,0:T(2,128)}), f32[256,2,512]{2,1,0:T(2,128)}) %all-reduce.11.cloned.1.call-update) | async-done | bytes 1048592
  (784 shorter events, 433.9 us)
Async XLA Ops:
  7.2 110.2 %all-gather.2.cloned.1.call-start = ((), (), s32[]{:S(2)}) async-start(), calls=%async_computation.8 | async-start | bytes 9437184 | tf_op jit(solution)/shard_map/all_gather | solution.py:244
  32.5 632.9 %reduce-scatter.9.cloned.1.call-start = ((), (), s32[]{:S(2)}) async-start(), calls=%async_computation.9 | async-start | bytes 9437184 | tf_op jit(solution)/shard_map/reduce_scatter | solution.py:163
  141.7 28.3 %collective-permute-start = (bf16[160,2048]{1,0:T(8,128)(2,1)S(1)}, bf16[160,2048]{1,0:T(8,128)(2,1)S(1)}, u32[]{:S(2)}, u32[]{:S(2)}) collective-permute-start(bf16[160,2048]{1,0:T(8,128)(2,1)S(1)} %slice.353), channel_id=1, source_target_pairs={{0,1},{1,0},{2,3},{3,2},{4,5},{5,4},{6,7},{7,6},{8,9},{9,8},{10,11... | collective-permute-start | bytes 1966088 | tf_op jit(solution)/shard_map/ppermute | solution.py:92
  142.3 27.7 %collective-permute-start.3 = (bf16[160,2048]{1,0:T(8,128)(2,1)S(1)}, bf16[160,2048]{1,0:T(8,128)(2,1)S(1)}, u32[]{:S(2)}, u32[]{:S(2)}) collective-permute-start(bf16[160,2048]{1,0:T(8,128)(2,1)S(1)} %slice.357), channel_id=1, source_target_pairs={{0,2},{1,3},{2,0},{3,1},{4,6},{5,7},{6,4},{7,5},{8,10},{9,11},{10,... | collective-permute-start | bytes 1966088 | tf_op jit(solution)/shard_map/ppermute | solution.py:92
  154.1 28.9 %collective-permute-start.5 = (bf16[160,2048]{1,0:T(8,128)(2,1)S(1)}, bf16[160,2048]{1,0:T(8,128)(2,1)S(1)}, u32[]{:S(2)}, u32[]{:S(2)}) collective-permute-start(bf16[160,2048]{1,0:T(8,128)(2,1)S(1)} %add_convert_fusion.7), channel_id=1, source_target_pairs={{0,1},{1,0},{2,3},{3,2},{4,5},{5,4},{6,7},{7,6},{8,9},{9,8},{10,11... | collective-permute-start | bytes 1966088 | tf_op jit(solution)/shard_map/ppermute | solution.py:92
  156.2 26.9 %collective-permute-start.2 = (bf16[160,2048]{1,0:T(8,128)(2,1)S(1)}, bf16[160,2048]{1,0:T(8,128)(2,1)S(1)}, u32[]{:S(2)}, u32[]{:S(2)}) collective-permute-start(bf16[160,2048]{1,0:T(8,128)(2,1)S(1)} %add_convert_fusion.8), channel_id=1, source_target_pairs={{0,2},{1,3},{2,0},{3,1},{4,6},{5,7},{6,4},{7,5},{8,10},{9,11},{10,... | collective-permute-start | bytes 1966088 | tf_op jit(solution)/shard_map/ppermute | solution.py:92
  190.5 29.8 %collective-permute-start.6 = (bf16[320,2048]{1,0:T(8,128)(2,1)S(1)}, bf16[320,2048]{1,0:T(8,128)(2,1)S(1)}, u32[]{:S(2)}, u32[]{:S(2)}) collective-permute-start(bf16[320,2048]{1,0:T(8,128)(2,1)S(1)} %get-tuple-element.141), channel_id=1, source_target_pairs={{0,1},{1,0},{2,3},{3,2},{4,5},{5,4},{6,7},{7,6},{8,9},{9,8},{10,11... | collective-permute-start | bytes 3932168 | tf_op jit(solution)/shard_map/ppermute | solution.py:92
  192.0 29.7 %collective-permute-start.8 = (bf16[320,2048]{1,0:T(8,128)(2,1)S(1)}, bf16[320,2048]{1,0:T(8,128)(2,1)S(1)}, u32[]{:S(2)}, u32[]{:S(2)}) collective-permute-start(bf16[320,2048]{1,0:T(8,128)(2,1)S(1)} %get-tuple-element.141), channel_id=1, source_target_pairs={{0,2},{1,3},{2,0},{3,1},{4,6},{5,7},{6,4},{7,5},{8,10},{9,11},{10,... | collective-permute-start | bytes 3932168 | tf_op jit(solution)/shard_map/ppermute | solution.py:92
  220.3 33.2 %collective-permute-start.9 = (bf16[160,2048]{1,0:T(8,128)(2,1)S(1)}, bf16[160,2048]{1,0:T(8,128)(2,1)S(1)}, u32[]{:S(2)}, u32[]{:S(2)}) collective-permute-start(bf16[160,2048]{1,0:T(8,128)(2,1)S(1)} %slice.363), channel_id=1, source_target_pairs={{0,2},{1,3},{2,0},{3,1},{4,6},{5,7},{6,4},{7,5},{8,10},{9,11},{10,... | collective-permute-start | bytes 1966088 | tf_op jit(solution)/shard_map/ppermute | solution.py:92
  221.8 32.0 %collective-permute-start.10 = (bf16[160,2048]{1,0:T(8,128)(2,1)S(1)}, bf16[160,2048]{1,0:T(8,128)(2,1)S(1)}, u32[]{:S(2)}, u32[]{:S(2)}) collective-permute-start(bf16[160,2048]{1,0:T(8,128)(2,1)S(1)} %slice.364), channel_id=1, source_target_pairs={{0,1},{1,0},{2,3},{3,2},{4,5},{5,4},{6,7},{7,6},{8,9},{9,8},{10,11... | collective-permute-start | bytes 1966088 | tf_op jit(solution)/shard_map/ppermute | solution.py:92
  237.6 60.4 %collective-permute-start.7 = (bf16[160,2048]{1,0:T(8,128)(2,1)S(1)}, bf16[160,2048]{1,0:T(8,128)(2,1)S(1)}, u32[]{:S(2)}, u32[]{:S(2)}) collective-permute-start(bf16[160,2048]{1,0:T(8,128)(2,1)S(1)} %slice.361), channel_id=1, source_target_pairs={{0,1},{1,0},{2,3},{3,2},{4,5},{5,4},{6,7},{7,6},{8,9},{9,8},{10,11... | collective-permute-start | bytes 1966088 | tf_op jit(solution)/shard_map/ppermute | solution.py:92
  274.6 17.7 %collective-permute-start.14 = (bf16[160,2048]{1,0:T(8,128)(2,1)S(1)}, bf16[160,2048]{1,0:T(8,128)(2,1)S(1)}, u32[]{:S(2)}, u32[]{:S(2)}) collective-permute-start(bf16[160,2048]{1,0:T(8,128)(2,1)S(1)} %get-tuple-element.181), channel_id=1, source_target_pairs={{0,2},{1,3},{2,0},{3,1},{4,6},{5,7},{6,4},{7,5},{8,10},{9,11},{10,... | collective-permute-start | bytes 1966088 | tf_op jit(solution)/shard_map/ppermute | solution.py:92
  275.4 17.9 %collective-permute-start.11 = (bf16[160,2048]{1,0:T(8,128)(2,1)S(1)}, bf16[160,2048]{1,0:T(8,128)(2,1)S(1)}, u32[]{:S(2)}, u32[]{:S(2)}) collective-permute-start(bf16[160,2048]{1,0:T(8,128)(2,1)S(1)} %get-tuple-element.180), channel_id=1, source_target_pairs={{0,1},{1,0},{2,3},{3,2},{4,5},{5,4},{6,7},{7,6},{8,9},{9,8},{10,11... | collective-permute-start | bytes 1966088 | tf_op jit(solution)/shard_map/ppermute | solution.py:92
  279.9 26.4 %collective-permute-start.13 = (bf16[160,2048]{1,0:T(8,128)(2,1)S(1)}, bf16[160,2048]{1,0:T(8,128)(2,1)S(1)}, u32[]{:S(2)}, u32[]{:S(2)}) collective-permute-start(bf16[160,2048]{1,0:T(8,128)(2,1)S(1)} %slice.367), channel_id=1, source_target_pairs={{0,2},{1,3},{2,0},{3,1},{4,6},{5,7},{6,4},{7,5},{8,10},{9,11},{10,... | collective-permute-start | bytes 1966088 | tf_op jit(solution)/shard_map/ppermute | solution.py:92
  293.5 23.1 %collective-permute-start.12 = (bf16[160,2048]{1,0:T(8,128)(2,1)S(1)}, bf16[160,2048]{1,0:T(8,128)(2,1)S(1)}, u32[]{:S(2)}, u32[]{:S(2)}) collective-permute-start(bf16[160,2048]{1,0:T(8,128)(2,1)S(1)} %add_convert_fusion.6), channel_id=1, source_target_pairs={{0,2},{1,3},{2,0},{3,1},{4,6},{5,7},{6,4},{7,5},{8,10},{9,11},{10,... | collective-permute-start | bytes 1966088 | tf_op jit(solution)/shard_map/ppermute | solution.py:92
  330.1 27.5 %collective-permute-start.16 = (bf16[320,2048]{1,0:T(8,128)(2,1)S(1)}, bf16[320,2048]{1,0:T(8,128)(2,1)S(1)}, u32[]{:S(2)}, u32[]{:S(2)}) collective-permute-start(bf16[320,2048]{1,0:T(8,128)(2,1)S(1)} %get-tuple-element.139), channel_id=1, source_target_pairs={{0,1},{1,0},{2,3},{3,2},{4,5},{5,4},{6,7},{7,6},{8,9},{9,8},{10,11... | collective-permute-start | bytes 3932168 | tf_op jit(solution)/shard_map/ppermute | solution.py:92
  331.0 29.7 %collective-permute-start.18 = (bf16[320,2048]{1,0:T(8,128)(2,1)S(1)}, bf16[320,2048]{1,0:T(8,128)(2,1)S(1)}, u32[]{:S(2)}, u32[]{:S(2)}) collective-permute-start(bf16[320,2048]{1,0:T(8,128)(2,1)S(1)} %get-tuple-element.139), channel_id=1, source_target_pairs={{0,2},{1,3},{2,0},{3,1},{4,6},{5,7},{6,4},{7,5},{8,10},{9,11},{10,... | collective-permute-start | bytes 3932168 | tf_op jit(solution)/shard_map/ppermute | solution.py:92
  357.7 50.7 %collective-permute-start.19 = (bf16[160,2048]{1,0:T(8,128)(2,1)S(1)}, bf16[160,2048]{1,0:T(8,128)(2,1)S(1)}, u32[]{:S(2)}, u32[]{:S(2)}) collective-permute-start(bf16[160,2048]{1,0:T(8,128)(2,1)S(1)} %slice.373), channel_id=1, source_target_pairs={{0,2},{1,3},{2,0},{3,1},{4,6},{5,7},{6,4},{7,5},{8,10},{9,11},{10,... | collective-permute-start | bytes 1966088 | tf_op jit(solution)/shard_map/ppermute | solution.py:92
  360.8 47.5 %collective-permute-start.20 = (bf16[160,2048]{1,0:T(8,128)(2,1)S(1)}, bf16[160,2048]{1,0:T(8,128)(2,1)S(1)}, u32[]{:S(2)}, u32[]{:S(2)}) collective-permute-start(bf16[160,2048]{1,0:T(8,128)(2,1)S(1)} %slice.374), channel_id=1, source_target_pairs={{0,1},{1,0},{2,3},{3,2},{4,5},{5,4},{6,7},{7,6},{8,9},{9,8},{10,11... | collective-permute-start | bytes 1966088 | tf_op jit(solution)/shard_map/ppermute | solution.py:92
  386.0 73.9 %collective-permute-start.17 = (bf16[160,2048]{1,0:T(8,128)(2,1)S(1)}, bf16[160,2048]{1,0:T(8,128)(2,1)S(1)}, u32[]{:S(2)}, u32[]{:S(2)}) collective-permute-start(bf16[160,2048]{1,0:T(8,128)(2,1)S(1)} %slice.371), channel_id=1, source_target_pairs={{0,1},{1,0},{2,3},{3,2},{4,5},{5,4},{6,7},{7,6},{8,9},{9,8},{10,11... | collective-permute-start | bytes 1966088 | tf_op jit(solution)/shard_map/ppermute | solution.py:92
  441.9 23.3 %collective-permute-start.23 = (bf16[160,2048]{1,0:T(8,128)(2,1)S(1)}, bf16[160,2048]{1,0:T(8,128)(2,1)S(1)}, u32[]{:S(2)}, u32[]{:S(2)}) collective-permute-start(bf16[160,2048]{1,0:T(8,128)(2,1)S(1)} %slice.377), channel_id=1, source_target_pairs={{0,2},{1,3},{2,0},{3,1},{4,6},{5,7},{6,4},{7,5},{8,10},{9,11},{10,... | collective-permute-start | bytes 1966088 | tf_op jit(solution)/shard_map/ppermute | solution.py:92
  453.0 19.3 %collective-permute-start.22 = (bf16[160,2048]{1,0:T(8,128)(2,1)S(1)}, bf16[160,2048]{1,0:T(8,128)(2,1)S(1)}, u32[]{:S(2)}, u32[]{:S(2)}) collective-permute-start(bf16[160,2048]{1,0:T(8,128)(2,1)S(1)} %add_convert_fusion.4), channel_id=1, source_target_pairs={{0,2},{1,3},{2,0},{3,1},{4,6},{5,7},{6,4},{7,5},{8,10},{9,11},{10,... | collective-permute-start | bytes 1966088 | tf_op jit(solution)/shard_map/ppermute | solution.py:92
  481.6 23.9 %collective-permute-start.30 = (bf16[320,2048]{1,0:T(8,128)(2,1)}, bf16[320,2048]{1,0:T(8,128)(2,1)}, u32[]{:S(2)}, u32[]{:S(2)}) collective-permute-start(bf16[320,2048]{1,0:T(8,128)(2,1)} %get-tuple-element.143), channel_id=1, source_target_pairs={{0,1},{1,0},{2,3},{3,2},{4,5},{5,4},{6,7},{7,6},{8,9},{9,8},{10,11... | collective-permute-start | bytes 3932168 | tf_op jit(solution)/shard_map/ppermute | solution.py:92
  482.2 28.9 %collective-permute-start.31 = (bf16[320,2048]{1,0:T(8,128)(2,1)}, bf16[320,2048]{1,0:T(8,128)(2,1)}, u32[]{:S(2)}, u32[]{:S(2)}) collective-permute-start(bf16[320,2048]{1,0:T(8,128)(2,1)} %get-tuple-element.143), channel_id=1, source_target_pairs={{0,2},{1,3},{2,0},{3,1},{4,6},{5,7},{6,4},{7,5},{8,10},{9,11},{10,... | collective-permute-start | bytes 3932168 | tf_op jit(solution)/shard_map/ppermute | solution.py:92
  507.4 36.9 %collective-permute-start.32 = (bf16[160,2048]{1,0:T(8,128)(2,1)}, bf16[160,2048]{1,0:T(8,128)(2,1)}, u32[]{:S(2)}, u32[]{:S(2)}) collective-permute-start(bf16[160,2048]{1,0:T(8,128)(2,1)} %slice.382), channel_id=1, source_target_pairs={{0,2},{1,3},{2,0},{3,1},{4,6},{5,7},{6,4},{7,5},{8,10},{9,11},{10,... | collective-permute-start | bytes 1966088 | tf_op jit(solution)/shard_map/ppermute | solution.py:92
  513.1 31.3 %collective-permute-start.33 = (bf16[160,2048]{1,0:T(8,128)(2,1)}, bf16[160,2048]{1,0:T(8,128)(2,1)}, u32[]{:S(2)}, u32[]{:S(2)}) collective-permute-start(bf16[160,2048]{1,0:T(8,128)(2,1)} %slice.383), channel_id=1, source_target_pairs={{0,1},{1,0},{2,3},{3,2},{4,5},{5,4},{6,7},{7,6},{8,9},{9,8},{10,11... | collective-permute-start | bytes 1966088 | tf_op jit(solution)/shard_map/ppermute | solution.py:92
  577.6 314.4 %reduce-scatter.11.cloned.1.call-start = ((), (), s32[]{:S(2)}) async-start(), calls=%async_computation.10 | async-start | bytes 2985984 | tf_op jit(solution)/shard_map/reduce_scatter | solution.py:163
  684.4 41.4 %collective-permute-start.34 = (bf16[160,2048]{1,0:T(8,128)(2,1)}, bf16[160,2048]{1,0:T(8,128)(2,1)}, u32[]{:S(2)}, u32[]{:S(2)}) collective-permute-start(bf16[160,2048]{1,0:T(8,128)(2,1)} %slice.395), channel_id=1, source_target_pairs={{0,1},{1,0},{2,3},{3,2},{4,5},{5,4},{6,7},{7,6},{8,9},{9,8},{10,11... | collective-permute-start | bytes 1966088 | tf_op jit(solution)/shard_map/ppermute | solution.py:92
  685.9 30.4 %collective-permute-start.35 = (bf16[160,2048]{1,0:T(8,128)(2,1)S(1)}, bf16[160,2048]{1,0:T(8,128)(2,1)S(1)}, u32[]{:S(2)}, u32[]{:S(2)}) collective-permute-start(bf16[160,2048]{1,0:T(8,128)(2,1)S(1)} %get-tuple-element.172), channel_id=1, source_target_pairs={{0,1},{1,0},{2,3},{3,2},{4,5},{5,4},{6,7},{7,6},{8,9},{9,8},{10,11... | collective-permute-start | bytes 1966088 | tf_op jit(solution)/shard_map/ppermute | solution.py:92
  688.3 37.5 %collective-permute-start.37 = (bf16[160,2048]{1,0:T(8,128)(2,1)}, bf16[160,2048]{1,0:T(8,128)(2,1)}, u32[]{:S(2)}, u32[]{:S(2)}) collective-permute-start(bf16[160,2048]{1,0:T(8,128)(2,1)} %slice.399), channel_id=1, source_target_pairs={{0,2},{1,3},{2,0},{3,1},{4,6},{5,7},{6,4},{7,5},{8,10},{9,11},{10,... | collective-permute-start | bytes 1966088 | tf_op jit(solution)/shard_map/ppermute | solution.py:92
  699.8 27.6 %collective-permute-start.39 = (bf16[160,2048]{1,0:T(8,128)(2,1)}, bf16[160,2048]{1,0:T(8,128)(2,1)}, u32[]{:S(2)}, u32[]{:S(2)}) collective-permute-start(bf16[160,2048]{1,0:T(8,128)(2,1)} %add_convert_fusion.1), channel_id=1, source_target_pairs={{0,1},{1,0},{2,3},{3,2},{4,5},{5,4},{6,7},{7,6},{8,9},{9,8},{10,11... | collective-permute-start | bytes 1966088 | tf_op jit(solution)/shard_map/ppermute | solution.py:92
  745.8 150.5 %reduce-scatter.15.cloned.1.call-start = ((), (), s32[]{:S(2)}) async-start(), calls=%async_computation.12 | async-start | bytes 2359296 | tf_op jit(solution)/shard_map/reduce_scatter | solution.py:163
  754.2 177.1 %reduce-scatter.17.cloned.1.call-start = ((), (), s32[]{:S(2)}) async-start(), calls=%async_computation.13 | async-start | bytes 2359296 | tf_op jit(solution)/shard_map/reduce_scatter | solution.py:163
  774.3 158.8 %reduce-scatter.13.cloned.1.call-start = ((), (), s32[]{:S(2)}) async-start(), calls=%async_computation.11 | async-start | bytes 2359296 | tf_op jit(solution)/shard_map/reduce_scatter | solution.py:163
  782.0 208.4 %reduce-scatter.23.cloned.1.call-start = ((), (), s32[]{:S(2)}) async-start(), calls=%async_computation.16 | async-start | bytes 9437184 | tf_op jit(solution)/shard_map/reduce_scatter | solution.py:163
  804.0 276.7 %reduce-scatter.21.cloned.1.call-start = ((), (), s32[]{:S(2)}) async-start(), calls=%async_computation.15 | async-start | bytes 9437184 | tf_op jit(solution)/shard_map/reduce_scatter | solution.py:163
  821.9 349.1 %reduce-scatter.19.cloned.1.call-start = ((), (), s32[]{:S(2)}) async-start(), calls=%async_computation.14 | async-start | bytes 9437184 | tf_op jit(solution)/shard_map/reduce_scatter | solution.py:163
  839.8 393.6 %all-reduce.11.cloned.1.call-start = ((), (), s32[]{:S(2)}) async-start(), calls=%async_computation.17 | async-start | bytes 2097152
  854.9 31.7 %collective-permute-start.26 = (bf16[320,2048]{1,0:T(8,128)(2,1)S(1)}, bf16[320,2048]{1,0:T(8,128)(2,1)S(1)}, u32[]{:S(2)}, u32[]{:S(2)}) collective-permute-start(bf16[320,2048]{1,0:T(8,128)(2,1)S(1)} %copy-done.46), channel_id=1, source_target_pairs={{0,1},{1,0},{2,3},{3,2},{4,5},{5,4},{6,7},{7,6},{8,9},{9,8},{10,11... | collective-permute-start | bytes 3932168 | tf_op jit(solution)/shard_map/ppermute | solution.py:92
  855.5 32.6 %collective-permute-start.27 = (bf16[320,2048]{1,0:T(8,128)(2,1)S(1)}, bf16[320,2048]{1,0:T(8,128)(2,1)S(1)}, u32[]{:S(2)}, u32[]{:S(2)}) collective-permute-start(bf16[320,2048]{1,0:T(8,128)(2,1)S(1)} %copy-done.46), channel_id=1, source_target_pairs={{0,2},{1,3},{2,0},{3,1},{4,6},{5,7},{6,4},{7,5},{8,10},{9,11},{10,... | collective-permute-start | bytes 3932168 | tf_op jit(solution)/shard_map/ppermute | solution.py:92
  863.8 310.0 %collective-permute-start.40 = (bf16[320,2048]{1,0:T(8,128)(2,1)}, bf16[320,2048]{1,0:T(8,128)(2,1)}, u32[]{:S(2)}, u32[]{:S(2)}) collective-permute-start(bf16[320,2048]{1,0:T(8,128)(2,1)} %get-tuple-element.147), channel_id=1, source_target_pairs={{0,1},{1,0},{2,3},{3,2},{4,5},{5,4},{6,7},{7,6},{8,9},{9,8},{10,11... | collective-permute-start | bytes 3932168 | tf_op jit(solution)/shard_map/ppermute | solution.py:92
  865.1 311.4 %collective-permute-start.41 = (bf16[320,2048]{1,0:T(8,128)(2,1)}, bf16[320,2048]{1,0:T(8,128)(2,1)}, u32[]{:S(2)}, u32[]{:S(2)}) collective-permute-start(bf16[320,2048]{1,0:T(8,128)(2,1)} %get-tuple-element.147), channel_id=1, source_target_pairs={{0,2},{1,3},{2,0},{3,1},{4,6},{5,7},{6,4},{7,5},{8,10},{9,11},{10,... | collective-permute-start | bytes 3932168 | tf_op jit(solution)/shard_map/ppermute | solution.py:92
  887.5 36.3 %collective-permute-start.28 = (bf16[160,2048]{1,0:T(8,128)(2,1)}, bf16[160,2048]{1,0:T(8,128)(2,1)}, u32[]{:S(2)}, u32[]{:S(2)}) collective-permute-start(bf16[160,2048]{1,0:T(8,128)(2,1)} %slice.380), channel_id=1, source_target_pairs={{0,2},{1,3},{2,0},{3,1},{4,6},{5,7},{6,4},{7,5},{8,10},{9,11},{10,... | collective-permute-start | bytes 1966088 | tf_op jit(solution)/shard_map/ppermute | solution.py:92
  890.0 38.8 %collective-permute-start.29 = (bf16[160,2048]{1,0:T(8,128)(2,1)}, bf16[160,2048]{1,0:T(8,128)(2,1)}, u32[]{:S(2)}, u32[]{:S(2)}) collective-permute-start(bf16[160,2048]{1,0:T(8,128)(2,1)} %slice.381), channel_id=1, source_target_pairs={{0,1},{1,0},{2,3},{3,2},{4,5},{5,4},{6,7},{7,6},{8,9},{9,8},{10,11... | collective-permute-start | bytes 1966088 | tf_op jit(solution)/shard_map/ppermute | solution.py:92
  893.8 285.3 %collective-permute-start.48 = (f32[256,648]{0,1:T(8,128)}, f32[256,648]{0,1:T(8,128)}, u32[]{:S(2)}, u32[]{:S(2)}) collective-permute-start(f32[256,648]{0,1:T(8,128)} %convert_element_type.518), channel_id=1, source_target_pairs={{0,1},{1,0},{2,3},{3,2},{4,5},{5,4},{6,7},{7,6},{8,9},{9,8},{10,11... | collective-permute-start | bytes 1990664 | tf_op jit(solution)/shard_map/ppermute | solution.py:92
  1174.9 23.3 %collective-permute-start.42 = (bf16[160,2048]{1,0:T(8,128)(2,1)S(1)}, bf16[160,2048]{1,0:T(8,128)(2,1)S(1)}, u32[]{:S(2)}, u32[]{:S(2)}) collective-permute-start(bf16[160,2048]{1,0:T(8,128)(2,1)S(1)} %slice.402), channel_id=1, source_target_pairs={{0,2},{1,3},{2,0},{3,1},{4,6},{5,7},{6,4},{7,5},{8,10},{9,11},{10,... | collective-permute-start | bytes 1966088 | tf_op jit(solution)/shard_map/ppermute | solution.py:92
  1177.6 20.6 %collective-permute-start.43 = (bf16[160,2048]{1,0:T(8,128)(2,1)S(1)}, bf16[160,2048]{1,0:T(8,128)(2,1)S(1)}, u32[]{:S(2)}, u32[]{:S(2)}) collective-permute-start(bf16[160,2048]{1,0:T(8,128)(2,1)S(1)} %slice.403), channel_id=1, source_target_pairs={{0,1},{1,0},{2,3},{3,2},{4,5},{5,4},{6,7},{7,6},{8,9},{9,8},{10,11... | collective-permute-start | bytes 1966088 | tf_op jit(solution)/shard_map/ppermute | solution.py:92
  1180.3 55.6 %collective-permute-start.49 = (f32[256,648]{0,1:T(8,128)S(1)}, f32[256,648]{0,1:T(8,128)S(1)}, u32[]{:S(2)}, u32[]{:S(2)}) collective-permute-start(f32[256,648]{0,1:T(8,128)S(1)} %convert_add_fusion.10), channel_id=1, source_target_pairs={{0,2},{1,3},{2,0},{3,1},{4,6},{5,7},{6,4},{7,5},{8,10},{9,11},{10,... | collective-permute-start | bytes 1990664 | tf_op jit(solution)/shard_map/ppermute | solution.py:92
  (218 other events, 1691.4 us)
Sparse Core Ops, SparseCore 0:
  32.7 84.7 all-gather.1
  577.7 87.6 reduce-scatter.8
  745.9 41.1 reduce-scatter.10
  789.8 35.3 reduce-scatter.14
  827.9 34.5 reduce-scatter.16
  865.2 34.6 reduce-scatter.12
  902.2 88.1 reduce-scatter.22
  992.6 87.9 reduce-scatter.20
  1083.0 87.9 reduce-scatter.18
  1173.9 59.5 all-reduce.10
